TPU v7x, 32 devices: a whole 2x2x4 slice. The times are simulated.
32 devices in a mesh: gx: 2 (over y), gy: 4 (over x, core), gz: 4 (over z).
Axes of the slice: x: 2, y: 2, z: 4, core: 2. Of those that a mesh axis runs over, the one named last changes fastest.
Arguments:
- features: bfloat16 [6, 8, 32, 8, 128], P('gx', 'gy', 'gz'), may hold values from -6 to 6
- positions: float32 [6, 8, 32, 24], P('gx', 'gy', 'gz'), may hold values from 0 to 256, as said below
- grid_anchor: int32 [6, 8, 32, 24], P('gx', 'gy', 'gz'), may hold values from -1 to 254, as said below
- species: int32 [6, 8, 32, 8], P('gx', 'gy', 'gz'), may hold values from 0 to 1
- neighbours: int32 [6, 8, 32, 512], P('gx', 'gy', 'gz'), may hold values from 0 to 12287, as said below
- neighbour_count: int32 [6, 8, 32, 8], P('gx', 'gy', 'gz'), may hold values from 32 to 64
- w_self: bfloat16 [128, 128], replicated, may hold values from -0.5 to 0.5
- w_neighbour: bfloat16 [128, 128], replicated, may hold values from -0.5 to 0.5
- w_radial: bfloat16 [8, 128], replicated, may hold values from -2 to 2
- radial_rates: float32 [8], replicated, may hold values from 0.05 to 2
- w_pair1: bfloat16 [128, 128], replicated, may hold values from -0.5 to 0.5
- w_pair2: bfloat16 [128, 128], replicated, may hold values from -0.5 to 0.5
- w_vector: bfloat16 [128, 128], replicated, may hold values from -0.5 to 0.5
- w_out: bfloat16 [128, 128], replicated, may hold values from -0.5 to 0.5
- w_charge: bfloat16 [128], replicated, may hold values from -0.5 to 0.5
- species_charge: float32 [2], replicated, may hold values from -1 to 1
Outputs:
- features_out: bfloat16 [6, 8, 32, 8, 128], P('gx', 'gy', 'gz')
- site_potential: float32 [6, 8, 32, 8], P('gx', 'gy', 'gz')
Inputs may be any that keep to these rules, and one draw needn't show every extreme that they name: `positions`: component d of slot s of cell (cx, cy, cz) lies in that cell: between c_d * 8 and (c_d + 1) * 8. `grid_anchor`: at the same place as in positions, the whole part of the coordinate minus 1; the coordinate lies between grid_anchor + 1 and grid_anchor + 2. `neighbours`: each entry is the index ((cx * 8 + cy) * 32 + cz) * 8 + s of an atom whose cell differs from the listing atom's cell by at most one along each dimension, periodically; never the listing atom itself.
All inputs are finite; a program needn't handle non-finite values.
Results may differ from a plain program's by a relative error of at most 0.0039.
The roundings to bfloat16 on the way count: a program that leaves them out, or rounds other values in their place, can miss the bound.
Values may be sent and summed in bfloat16 or wider, within the bound.
A program may use at most 64 MiB of HBM per device.

v0:
```python
import functools
import math

import jax
import jax.numpy as jnp
import numpy as np
from jax import lax
from jax.experimental import pallas as pl
from jax.experimental.pallas import tpu as pltpu
from jax.sharding import PartitionSpec as P

NBR = 64
CELL = 8
AXES = ("gx", "gy", "gz")

coulomb_scale = 0.25
smearing = 1.0
highest = lax.Precision.HIGHEST


def round_bf16(x):
    return lax.reduce_precision(x, 8, 7)


def three_pieces(x):
    hi = round_bf16(x)
    mid = round_bf16(x - hi)
    lo = round_bf16(x - hi - mid)
    return hi, mid, lo


def cast_pieces(x, count):
    pieces = []
    for _ in range(count):
        piece = x.astype(jnp.bfloat16)
        pieces.append(piece)
        x = x - piece.astype(jnp.float32)
    return pieces


def silu(v):
    half = 0.5 * v
    return half + half * jnp.tanh(half)


def pair_kernel(
    cells,
    lengths,
    code_ref,
    ext_ref,
    own_ref,
    hidden_ref,
    wr_ref,
    rates_ref,
    w1_ref,
    w2_ref,
    wv_ref,
    wo_ref,
    out_ref,
    msg_ref,
    vec_ref,
    w1t_ref,
    w2t_ref,
):
    cells_x, cells_y, cells_z = cells
    f32, bf16 = jnp.float32, jnp.bfloat16
    slots = 8
    pairs = slots * NBR
    w1t_ref[...] = w1_ref[...].astype(f32).T.astype(bf16)
    w2t_ref[...] = w2_ref[...].astype(f32).T.astype(bf16)
    wr_rows = jnp.concatenate([wr_ref[...].astype(f32), jnp.zeros((8, 128), f32)], axis=1)
    zero_half = jnp.zeros((8, 128), f32)
    lane_slot = lax.broadcasted_iota(jnp.int32, (slots, pairs), 1) // NBR
    sel = jnp.where(lane_slot == lax.broadcasted_iota(jnp.int32, (slots, pairs), 0), 1.0, 0.0)
    tail = jnp.concatenate([sel, sel, sel, jnp.zeros((8, pairs), f32)], axis=0).astype(bf16)
    row_d = lax.broadcasted_iota(jnp.int32, (8, 1), 0)
    box = jnp.where(
        row_d == 0,
        float(lengths[0]),
        jnp.where(row_d == 1, float(lengths[1]), float(lengths[2])),
    )
    box_inv = 1.0 / box
    rates = rates_ref[...]

    def one_cell(c, carry):
        cz = c % cells_z
        cxy = c // cells_z
        cy = cxy % cells_y
        cx = cxy // cells_y
        row = pl.multiple_of(cz * 8, 8)
        here = pl.multiple_of(c * 8, 8)
        parts = []
        for dx in range(3):
            for dy in range(3):
                column = (cx + dx) * (cells_y + 2) + cy + dy
                parts.append(ext_ref[column, pl.ds(row, 24), :])
        mine = ext_ref[(cx + 1) * (cells_y + 2) + cy + 1, pl.ds(row + 8, 8), 128:]
        own = own_ref[pl.ds(here, 8), :]
        own_hi, own_mid, own_lo = [p.astype(f32) for p in cast_pieces(own, 3)]
        parts.append(wr_rows)
        parts.append(jnp.concatenate([own_hi, -mine], axis=1))
        parts.append(jnp.concatenate([own_mid, zero_half], axis=1))
        parts.append(jnp.concatenate([own_lo, zero_half], axis=1))
        parts.append(jnp.zeros((8, 256), f32))
        table = jnp.concatenate(parts, axis=0)
        sent_t = table[:, :128].T.astype(bf16)
        place_t = table[:, 128:].T[:32].astype(bf16)
        code = code_ref[c]
        which = code & 255
        live = jnp.where(code < 256, 1.0, 0.0)
        hot = jnp.where(
            lax.broadcasted_iota(jnp.int32, (216, pairs), 0) == which, 1.0, 0.0
        )
        hot_main = hot[:208].astype(bf16)
        hot_last = hot[208:]
        rhs_place = jnp.concatenate(
            [
                hot_main,
                jnp.concatenate([hot_last, jnp.zeros((8, pairs), f32)], axis=0).astype(bf16),
                tail,
            ],
            axis=0,
        )
        found = jnp.dot(place_t, rhs_place, preferred_element_type=f32)
        displace = found[0:8] + found[8:16] + found[16:24]
        displace = displace - box * jnp.floor(displace * box_inv + 0.5)
        scaled = displace * (1.0 / CELL)
        square = jnp.sum(scaled * scaled, axis=0, keepdims=True)
        basis = jnp.exp(-square * rates)
        rhs = jnp.concatenate(
            [hot_main, jnp.concatenate([hot_last, basis], axis=0).astype(bf16), tail], axis=0
        )
        pre = jnp.dot(sent_t, rhs, preferred_element_type=f32)
        latent = silu(pre).astype(bf16)
        second = silu(jnp.dot(w1t_ref[...], latent, preferred_element_type=f32)).astype(bf16)
        third = silu(jnp.dot(w2t_ref[...], second, preferred_element_type=f32)).astype(bf16)
        reach = scaled * live
        pieces = [p.astype(f32) for p in cast_pieces(reach, 3)]
        rows = [sel * live]
        for d in range(3):
            for piece in pieces:
                rows.append(sel * piece[d : d + 1])
        weights = jnp.concatenate(rows, axis=0).astype(bf16)
        sums = lax.dot_general(
            weights, third, (((1,), (1,)), ((), ())), preferred_element_type=f32
        )
        msg_ref[pl.ds(here, 8), :] = sums[0:8] * (1.0 / NBR)
        for d in range(3):
            base = 8 + 24 * d
            vec_ref[d, pl.ds(here, 8), :] = (
                sums[base : base + 8] + sums[base + 8 : base + 16] + sums[base + 16 : base + 24]
            )
        return carry

    lax.fori_loop(0, cells_x * cells_y * cells_z, one_cell, 0, unroll=8)
    wv = wv_ref[...].astype(f32)
    invariant = None
    for d in range(3):
        vector = jnp.dot(
            vec_ref[d], wv, precision=highest, preferred_element_type=f32
        ) * (1.0 / math.sqrt(NBR))
        part = vector * vector
        invariant = part if invariant is None else invariant + part
    update = (msg_ref[...] + invariant).astype(bf16)
    out_ref[...] = (
        hidden_ref[...].astype(f32)
        + jnp.dot(update, wo_ref[...], preferred_element_type=f32)
    ).astype(bf16)


def spline(distance):
    outer = jnp.maximum(2.0 - distance, 0.0)
    inner = jnp.maximum(1.0 - distance, 0.0)
    return (outer * outer * outer - 4.0 * (inner * inner * inner)) * (1.0 / 6.0)


def trig_basis(length):
    r = np.arange(length)
    rows = [np.cos(2 * np.pi * ((k * r) % length) / length) for k in range(length // 2 + 1)]
    rows += [np.sin(2 * np.pi * ((k * r) % length) / length) for k in range(1, length // 2)]
    modes = np.array(list(range(length // 2 + 1)) + list(range(1, length // 2)))
    return np.stack(rows), modes


def axis_terms(modes, length):
    wave = modes * (2.0 * np.pi / length)
    turn = np.exp(2j * np.pi * modes / length)
    modulus = np.abs(1 / 6 + 4 / 6 * turn + 1 / 6 * turn * turn) ** 2
    weight = np.where((modes == 0) | (2 * modes == length), 1.0, 2.0) / length
    return wave * wave, weight / modulus


def charge_kernel(
    sizes,
    lengths,
    window,
    screen,
    planes,
    atoms_ref,
    zrow_ref,
    krow_ref,
    kx_ref,
    by_ref,
    byt_ref,
    bx_ref,
    bxt_ref,
    out_ref,
    plane_ref,
    wave_ref,
):
    devices_x, devices_y, devices_z = sizes
    length_x, length_y, length_z = lengths
    grid_y = length_y // devices_y
    f32, bf16 = jnp.float32, jnp.bfloat16
    lanes = atoms_ref.shape[-1] * devices_z

    def load(gx, gy):
        base = (gx * devices_y + gy) * devices_z
        return jnp.concatenate([atoms_ref[base + i] for i in range(devices_z)], axis=1)

    def stencils(atoms, gy):
        ids_x = lax.broadcasted_iota(jnp.int32, (length_x, lanes), 0).astype(f32)
        off_x = jnp.abs(ids_x - atoms[0:1])
        rows_x = spline(jnp.minimum(off_x, length_x - off_x))
        start = (gy * grid_y - 1).astype(f32)
        ids_y = lax.broadcasted_iota(jnp.int32, (window, lanes), 0).astype(f32)
        rows_y = spline(jnp.abs(ids_y - (atoms[1:2] - start)))
        return rows_x, rows_y

    zrow = zrow_ref[my_index(sizes)]

    def spread(gx, gy):
        atoms = load(gx, gy)
        rows_x, rows_y = stencils(atoms, gy)
        place_z = atoms[2:3]
        whole = jnp.floor(place_z)
        f = place_z - whole
        sq = f * f
        cube = sq * f
        rem = 1.0 - f
        taps = [
            rem * rem * rem * (1.0 / 6.0),
            (3.0 * cube - 6.0 * sq + 4.0) * (1.0 / 6.0),
            (-3.0 * cube + 3.0 * sq + 3.0 * f + 1.0) * (1.0 / 6.0),
            cube * (1.0 / 6.0),
        ]
        turns = zrow[:, 0:1] * (whole - 1.0)
        turns = turns - length_z * jnp.floor(turns * (1.0 / length_z))
        angle = (turns - 0.5 * length_z) * (2.0 * math.pi / length_z)
        cos_a = -jnp.cos(angle)
        sin_a = -jnp.sin(angle)
        shift_c = zrow[:, 1:2]
        shift_s = zrow[:, 2:3]
        base_c = cos_a * shift_c + sin_a * shift_s
        base_s = sin_a * shift_c - cos_a * shift_s
        even = taps[0]
        odd = 0.0
        for t in range(1, 4):
            even = even + taps[t] * zrow[:, 2 + t : 3 + t]
            odd = odd + taps[t] * zrow[:, 5 + t : 6 + t]
        wave = base_c * even - base_s * odd
        wave_ref[gx * devices_y + gy] = wave
        scaled = wave * atoms[3:4]
        left = jnp.concatenate([rows_y * scaled[j : j + 1] for j in range(planes)], axis=0)
        left_hi = left.astype(bf16)
        left_lo = (left - left_hi.astype(f32)).astype(bf16)
        x_hi = rows_x.astype(bf16)
        x_lo = (rows_x - x_hi.astype(f32)).astype(bf16)
        res = lax.dot_general(
            jnp.concatenate([left_hi, left_lo], axis=0),
            jnp.concatenate([x_hi, x_lo], axis=0),
            (((1,), (1,)), ((), ())),
            preferred_element_type=f32,
        )
        half = planes * window
        res = res[:half] + res[half:]
        return res[:, :length_x] + res[:, length_x:]

    plane_ref[...] = jnp.zeros(plane_ref.shape, f32)

    def spread_group(g, carry):
        gy = g % devices_y
        total = spread(g // devices_y, gy)
        rows = pl.ds(pl.multiple_of(gy * window, 8), window)
        for j in range(planes):
            plane_ref[j, rows, :] += total[j * window : (j + 1) * window]
        return carry

    lax.fori_loop(0, devices_x * devices_y, spread_group, 0, unroll=2)

    def hdot(a, b):
        return jnp.dot(a, b, precision=highest, preferred_element_type=f32)

    along_y = jnp.concatenate([hdot(by_ref[...], plane_ref[j]) for j in range(planes)], axis=0)
    spectrum = hdot(along_y, bxt_ref[...])
    kcol = krow_ref[...]
    filtered = []
    for j in range(planes):
        q = kcol[:, 0:1] + zrow[j : j + 1, 9:10] + kx_ref[0:1, :]
        scale = kcol[:, 1:2] * zrow[j : j + 1, 10:11] * kx_ref[1:2, :]
        green = (coulomb_scale * 4.0 * math.pi) * jnp.exp(-0.5 * smearing * smearing * q)
        green = green * scale / (q + 1.0 / (screen * screen))
        green = jnp.where(q == 0.0, 0.0, green)
        filtered.append(spectrum[j * length_y : (j + 1) * length_y] * green)
    back = hdot(jnp.concatenate(filtered, axis=0), bx_ref[...])
    for j in range(planes):
        plane_ref[j] = hdot(byt_ref[...], back[j * length_y : (j + 1) * length_y])

    def sample_group(g, carry):
        gy = g % devices_y
        rows = pl.ds(pl.multiple_of(gy * window, 8), window)
        field = jnp.concatenate([plane_ref[j, rows, :] for j in range(planes)], axis=0)
        f_hi, f_mid = [p.astype(f32) for p in cast_pieces(field, 2)]
        field3 = jnp.concatenate([f_hi, f_mid, f_hi], axis=1).astype(bf16)
        atoms = load(g // devices_y, gy)
        rows_x, rows_y = stencils(atoms, gy)
        x_hi = rows_x.astype(bf16)
        x_lo = (rows_x - x_hi.astype(f32)).astype(bf16)
        values = jnp.dot(
            field3, jnp.concatenate([x_hi, x_hi, x_lo], axis=0), preferred_element_type=f32
        )
        wave = wave_ref[g]
        mixed = values[0:window] * wave[0:1]
        for j in range(1, planes):
            mixed = mixed + values[j * window : (j + 1) * window] * wave[j : j + 1]
        line = jnp.sum(mixed * rows_y, axis=0, keepdims=True)
        count = atoms_ref.shape[-1]
        for i in range(devices_z):
            out_ref[g * devices_z + i] = line[:, i * count : (i + 1) * count]
        return carry

    lax.fori_loop(0, devices_x * devices_y, sample_group, 0, unroll=2)


def coords_of(index, sizes):
    return (
        index // (sizes[1] * sizes[2]),
        (index // sizes[2]) % sizes[1],
        index % sizes[2],
    )


def my_index(sizes):
    gx, gy, gz = (lax.axis_index(a) for a in AXES)
    return (gx * sizes[1] + gy) * sizes[2] + gz


def gather_kernel(
    sizes, cells, atoms_ref, rows_ref, all_ref, ext_ref, asend, arecv, hsend, hrecv, local_sem
):
    devices = sizes[0] * sizes[1] * sizes[2]
    here = tuple(lax.axis_index(a) for a in AXES)
    me = my_index(sizes)
    copies = []
    for shift in range(27):
        step = (shift // 9 - 1, shift // 3 % 3 - 1, shift % 3 - 1)
        if step == (0, 0, 0):
            continue
        source, target, peer = [], [], []
        for axis in range(3):
            size = cells[axis]
            if step[axis] == 0:
                source.append(pl.ds(0, size))
                target.append(pl.ds(1, size))
                peer.append(here[axis])
            elif step[axis] > 0:
                source.append(pl.ds(size - 1, 1))
                target.append(pl.ds(0, 1))
                peer.append(lax.rem(here[axis] + 1, sizes[axis]))
            else:
                source.append(pl.ds(0, 1))
                target.append(pl.ds(size + 1, 1))
                peer.append(lax.rem(here[axis] + sizes[axis] - 1, sizes[axis]))
        copy = pltpu.make_async_remote_copy(
            src_ref=rows_ref.at[tuple(source)],
            dst_ref=ext_ref.at[tuple(target)],
            send_sem=hsend.at[shift],
            recv_sem=hrecv.at[shift],
            device_id=tuple(peer),
            device_id_type=pl.DeviceIdType.MESH,
        )
        copies.append(copy)

    def atom_copy(o):
        peer = lax.rem(me + o, devices)
        return pltpu.make_async_remote_copy(
            src_ref=atoms_ref,
            dst_ref=all_ref.at[me],
            send_sem=asend.at[o],
            recv_sem=arecv.at[o],
            device_id=coords_of(peer, sizes),
            device_id_type=pl.DeviceIdType.MESH,
        )

    def start(o, carry):
        atom_copy(o).start()
        return carry

    lax.fori_loop(1, devices, start, 0)
    for copy in copies:
        copy.start()
    inner = tuple(pl.ds(1, size) for size in cells)
    local = pltpu.make_async_copy(rows_ref, ext_ref.at[inner], local_sem.at[0])
    local.start()
    local_atoms = pltpu.make_async_copy(atoms_ref, all_ref.at[me], local_sem.at[1])
    local_atoms.start()
    local.wait()
    local_atoms.wait()

    def finish(o, carry):
        origin = lax.rem(me + devices - o, devices)
        pltpu.make_async_remote_copy(
            src_ref=atoms_ref,
            dst_ref=all_ref.at[origin],
            send_sem=asend.at[o],
            recv_sem=arecv.at[o],
            device_id=coords_of(origin, sizes),
            device_id_type=pl.DeviceIdType.MESH,
        ).wait()
        return carry

    lax.fori_loop(1, devices, finish, 0)
    for copy in copies:
        copy.wait()


def scatter_kernel(sizes, part_ref, out_ref, held_ref, send, recv):
    devices = sizes[0] * sizes[1] * sizes[2]
    me = my_index(sizes)

    def copy_to(o):
        peer = lax.rem(me + o, devices)
        return pltpu.make_async_remote_copy(
            src_ref=part_ref.at[peer],
            dst_ref=held_ref.at[o],
            send_sem=send.at[o],
            recv_sem=recv.at[o],
            device_id=coords_of(peer, sizes),
            device_id_type=pl.DeviceIdType.MESH,
        )

    def start(o, carry):
        copy_to(o).start()
        return carry

    lax.fori_loop(1, devices, start, 0)

    def finish(o, total):
        copy_to(o).wait()
        return total + held_ref[o]

    out_ref[...] = lax.fori_loop(1, devices, finish, part_ref[me])


def shards(
    features,
    positions,
    grid_anchor,
    species,
    neighbours,
    neighbour_count,
    w_self,
    w_neighbour,
    w_radial,
    radial_rates,
    w_pair1,
    w_pair2,
    w_vector,
    w_out,
    w_charge,
    species_charge,
):
    f32, bf16 = jnp.float32, jnp.bfloat16
    cells_x, cells_y, cells_z, slot_count, channels = features.shape
    cell_count = cells_x * cells_y * cells_z
    atom_count = cell_count * slot_count
    sizes = tuple(lax.axis_size(a) for a in AXES)
    devices = sizes[0] * sizes[1] * sizes[2]
    totals = (cells_x * sizes[0], cells_y * sizes[1], cells_z * sizes[2])
    lengths = tuple(t * CELL for t in totals)
    length_x, length_y, length_z = lengths
    screen = 2 * cells_y * CELL

    hidden = features.reshape(atom_count, channels)
    own = jnp.dot(hidden, w_self, preferred_element_type=f32)
    sent = jnp.dot(hidden, w_neighbour, preferred_element_type=f32).astype(bf16)
    species_rows = species.reshape(atom_count)
    kind_ids = jnp.arange(species_charge.shape[0], dtype=jnp.int32)
    base_charge = jnp.sum(
        jnp.where(species_rows[:, None] == kind_ids[None, :], species_charge[None, :], 0.0), axis=1
    )
    charge = base_charge + jnp.dot(hidden, w_charge, preferred_element_type=f32)
    place = positions.reshape(cell_count, 3, slot_count)
    place_cols = jnp.moveaxis(place, 1, 0).reshape(3, atom_count)
    atoms = jnp.concatenate([place_cols, charge[None]], axis=0)

    hi, mid, lo = three_pieces(jnp.moveaxis(place, 1, 2).reshape(atom_count, 3))
    gap = jnp.zeros((atom_count, 5), f32)
    place_rows = jnp.concatenate(
        [hi, gap, mid, gap, lo, gap, jnp.zeros((atom_count, channels - 24), f32)], axis=1
    ).astype(bf16)
    rows = jnp.concatenate([sent, place_rows], axis=1)
    rows = rows.reshape(cells_x, cells_y, cells_z, slot_count, 2 * channels)
    cells = (cells_x, cells_y, cells_z)
    vmem = pl.BlockSpec(memory_space=pltpu.VMEM)
    dma = pltpu.SemaphoreType.DMA
    atoms, ext = pl.pallas_call(
        functools.partial(gather_kernel, sizes, cells),
        out_shape=(
            jax.ShapeDtypeStruct((devices,) + atoms.shape, f32),
            jax.ShapeDtypeStruct(
                tuple(c + 2 for c in cells) + (slot_count, 2 * channels), bf16
            ),
        ),
        in_specs=[vmem] * 2,
        out_specs=(vmem, vmem),
        scratch_shapes=[dma((devices,)), dma((devices,)), dma((27,)), dma((27,)), dma((2,))],
        name="gather_atoms",
        compiler_params=pltpu.CompilerParams(has_side_effects=True),
    )(atoms, rows)
    ext = ext.astype(f32).reshape(
        (cells_x + 2) * (cells_y + 2), (cells_z + 2) * slot_count, 2 * channels
    )

    listed = neighbours.reshape(cells_x, cells_y, cells_z, slot_count * NBR)
    slot_ids = listed % slot_count
    cell_ids = listed // slot_count
    steps = []
    for axis, ids in enumerate(
        (cell_ids // (totals[2] * totals[1]), cell_ids // totals[2] % totals[1], cell_ids % totals[2])
    ):
        local = lax.broadcasted_iota(jnp.int32, listed.shape, axis)
        first = lax.axis_index(AXES[axis]) * (cells_x, cells_y, cells_z)[axis]
        steps.append((ids - first - local + 1 + totals[axis]) % totals[axis])
    code = ((steps[0] * 3 + steps[1]) * 3 + steps[2]) * slot_count + slot_ids
    counts = neighbour_count.reshape(cell_count, slot_count, 1)
    dead = jnp.arange(NBR, dtype=jnp.int32)[None, None, :] >= counts
    code = code.reshape(cell_count, slot_count, NBR) + jnp.where(dead, 256, 0)
    code = code.reshape(cell_count, 1, slot_count * NBR)

    vmem = pl.BlockSpec(memory_space=pltpu.VMEM)
    updated = pl.pallas_call(
        functools.partial(pair_kernel, (cells_x, cells_y, cells_z), lengths),
        out_shape=jax.ShapeDtypeStruct((atom_count, channels), bf16),
        in_specs=[vmem] * 10,
        out_specs=vmem,
        scratch_shapes=[
            pltpu.VMEM((atom_count, channels), f32),
            pltpu.VMEM((3, atom_count, channels), f32),
            pltpu.VMEM((channels, channels), bf16),
            pltpu.VMEM((channels, channels), bf16),
        ],
        name="pair_layer",
        cost_estimate=pl.CostEstimate(
            flops=2 * atom_count * NBR * channels * 512,
            bytes_accessed=4 * 1024 * 1024,
            transcendentals=3 * atom_count * NBR * channels,
        ),
    )(
        code,
        ext,
        own,
        hidden,
        w_radial,
        radial_rates.reshape(-1, 1),
        w_pair1,
        w_pair2,
        w_vector,
        w_out,
    )

    share = length_z // 2 // devices
    planes = 2 * share
    window = -(-(cells_y * CELL + 4) // 8) * 8
    all_modes = np.arange(length_z // 2)
    table_k = np.stack([all_modes, all_modes], axis=1)
    phase_c = np.stack([np.ones_like(all_modes), np.zeros_like(all_modes)], axis=1)
    table_k[0, 1] = length_z // 2
    phase_c[0, 1] = 1
    table_k = table_k.reshape(devices, planes)
    phase_c = phase_c.reshape(devices, planes).astype(np.float64)
    taps = [2 * np.pi * ((table_k * t) % length_z) / length_z for t in range(1, 4)]
    basis_x, modes_x = trig_basis(length_x)
    basis_y, modes_y = trig_basis(length_y)
    qx, sx = axis_terms(modes_x, length_x)
    qy, sy = axis_terms(modes_y, length_y)
    qz, sz = axis_terms(table_k, length_z)
    krow = np.stack([qy, sy], axis=1).astype(np.float32)
    zrow = np.stack(
        [table_k, phase_c, 1.0 - phase_c]
        + [np.cos(a) for a in taps]
        + [np.sin(a) for a in taps]
        + [qz, sz],
        axis=2,
    ).astype(np.float32)
    kx = np.stack([qx, sx]).astype(np.float32)
    grid_y = cells_y * CELL
    columns = np.concatenate(
        [(np.arange(window) + g * grid_y - 1) % length_y for g in range(sizes[1])]
    )
    by = basis_y[:, columns].astype(np.float32)
    bx = basis_x.astype(np.float32)
    partial = pl.pallas_call(
        functools.partial(charge_kernel, sizes, lengths, window, screen, planes),
        out_shape=jax.ShapeDtypeStruct((devices, 1, atom_count), f32),
        in_specs=[vmem] * 8,
        out_specs=vmem,
        scratch_shapes=[
            pltpu.VMEM((planes, sizes[1] * window, length_x), f32),
            pltpu.VMEM((sizes[0] * sizes[1], planes, sizes[2] * atom_count), f32),
        ],
        name="charge_solve",
        cost_estimate=pl.CostEstimate(
            flops=10**10, bytes_accessed=2 * 1024 * 1024, transcendentals=10**6
        ),
    )(
        atoms,
        jnp.asarray(zrow),
        jnp.asarray(krow),
        jnp.asarray(kx),
        jnp.asarray(by),
        jnp.asarray(np.ascontiguousarray(by.T)),
        jnp.asarray(bx),
        jnp.asarray(np.ascontiguousarray(bx.T)),
    )
    site_potential = pl.pallas_call(
        functools.partial(scatter_kernel, sizes),
        out_shape=jax.ShapeDtypeStruct((1, atom_count), f32),
        in_specs=[vmem],
        out_specs=vmem,
        scratch_shapes=[
            pltpu.VMEM((devices, 1, atom_count), f32),
            dma((devices,)),
            dma((devices,)),
        ],
        name="scatter_sum",
        compiler_params=pltpu.CompilerParams(has_side_effects=True),
    )(partial)
    return (
        updated.reshape(features.shape),
        site_potential.reshape(cells_x, cells_y, cells_z, slot_count),
    )


def solution(mesh):
    return jax.shard_map(
        shards,
        mesh=mesh,
        in_specs=(
            P("gx", "gy", "gz", None, None),
            P("gx", "gy", "gz", None),
            P("gx", "gy", "gz", None),
            P("gx", "gy", "gz", None),
            P("gx", "gy", "gz", None),
            P("gx", "gy", "gz", None),
            P(),
            P(),
            P(),
            P(),
            P(),
            P(),
            P(),
            P(),
            P(),
            P(),
        ),
        out_specs=(P("gx", "gy", "gz", None, None), P("gx", "gy", "gz", None)),
        check_vma=False,
    )
```

profile of v0, /device:TPU:1, one launch (start us, length us, event | category | flops | bytes accessed | tf_op | source)
XLA Modules:
  0.0 97.4 jit_solution(15021884596517508373)
XLA Ops:
  0.6 0.8 copy.33
  1.5 0.1 reshape.89
  1.7 0.1 reshape.92
  1.8 1.1 %convolution_convert_fusion = bf16[384,128]{0,1:T(8,128)(2,1)S(1)} fusion(bf16[384,128]{1,0:T(8,128)(2,1)} %bitcast.25, bf16[128,128]{1,0:T(8,128)(2,1)S(1)} %copy-done), kind=kOutput, calls=%fused_computation | convolution fusion | flops 12632064 | bytes 229376 | tf_op jit(solution)/shard_map/dot_general | solution.py:486
  3.0 0.1 concatenate.10
  3.1 0.8 copy.36
  4.0 1.0 %convolution_reduce_fusion = f32[384]{0:T(512)S(1)} fusion(bf16[384,128]{1,0:T(8,128)(2,1)} %bitcast.26, bf16[128]{0:T(256)(128)(2,1)} %param.36), kind=kOutput, calls=%fused_computation.1 | convolution fusion | flops 98304 | bytes 100096 | tf_op jit(solution)/shard_map/dot_general | solution.py:492
  5.0 0.8 eq.22
  5.8 0.7 fusion.25
  6.7 0.1 reshape.90
  6.8 0.6 pad_maximum_fusion.atoms_ref
  7.4 22.4 %gather_atoms.1 = (f32[32,4,384]{2,1,0:T(4,128)}, bf16[5,4,10,8,256]{4,3,2,1,0:T(8,128)(2,1)}) custom-call(f32[4,384]{1,0:T(4,128)} %pad_maximum_fusion.atoms_ref, bf16[3,2,8,8,256]{4,3,2,1,0:T(8,128)(2,1)} %bitcast.30), custom_call_target="tpu_custom_call" | custom-call | tf_op jit(solution)/shard_map/gather_atoms/pallas_call | solution.py:507
  29.9 2.6 %convert.21.ext_ref = f32[20,80,256]{2,1,0:T(8,128)} convert(bf16[20,80,256]{2,1,0:T(8,128)(2,1)} %bitcast.29) | non-fusion elementwise | flops 409600 | bytes 2457600 | tf_op jit(solution)/shard_map/reshape | solution.py:521
  32.4 0.4 fusion.10
  32.8 0.1 reshape.88
  33.1 0.2 ge.33
  33.3 0.8 fusion.20.code_ref
  34.1 0.8 fusion.27.own_ref
  34.9 0.7 copy.37.rates_ref
  35.6 33.5 %pair_layer.1 = bf16[384,128]{1,0:T(8,128)(2,1)} custom-call(s32[48,1,512]{2,1,0:T(1,128)} %fusion.20.code_ref, f32[20,80,256]{2,1,0:T(8,128)} %convert.21.ext_ref, f32[384,128]{1,0:T(8,128)} %fusion.27.own_ref, bf16[384,128]{1,0:T(8,128)(2,1)} %bitcast.27, bf16[8,128]{1,0:T(8,128)(2,1)} %wr_ref.1, f32[8,1]{1,0:T(8,128)} %copy.37.rates_ref, ...), custom_call_target="tpu_custom_call" | custom-call | flops 3221225472 | bytes 4194304 | tf_op jit(solution)/shard_map/pair_layer/pallas_call | solution.py:542
  69.1 14.3 %charge_solve.1.part_ref = f32[32,1,384]{2,1,0:T(1,128)} custom-call(f32[32,4,384]{2,1,0:T(4,128)} %get-tuple-element.5.atoms_ref, f32[32,8,11]{2,1,0:T(8,128)} %constant.129.clone.zrow_ref, f32[64,2]{1,0:T(8,128)} %constant.130.clone.krow_ref, f32[2,48]{1,0:T(2,128)} %constant.131.clone.kx_ref, f32[64,96]{1,0:T(8,128)} %constant.132.clone.by_ref, ...), custom_call_target="tpu_custom_call" | custom-call | flops 10000000000 | bytes 2097152 | tf_op jit(solution)/shard_map/charge_solve/pallas_call | solution.py:603
  83.3 12.6 %scatter_sum.1 = f32[1,384]{1,0:T(1,128)} custom-call(f32[32,1,384]{2,1,0:T(1,128)} %charge_solve.1.part_ref), custom_call_target="tpu_custom_call" | custom-call | tf_op jit(solution)/shard_map/scatter_sum/pallas_call | solution.py:626
  96.0 0.7 reduce.1
  96.7 0.7 reshape.98
  (22 shorter events, 0.4 us)
Async XLA Ops:
  0.6 1.2 %copy-start = (bf16[128,128]{1,0:T(8,128)(2,1)S(1)}, bf16[128,128]{1,0:T(8,128)(2,1)}, u32[]{:S(2)}) copy-start(bf16[128,128]{1,0:T(8,128)(2,1)} %param.29) | copy-start | bytes 98308
  3.1 29.3 %copy-start.2 = (s32[3,2,8,512]{3,2,1,0:T(8,128)S(1)}, s32[3,2,8,512]{3,2,1,0:T(8,128)}, u32[]{:S(2)}) copy-start(s32[3,2,8,512]{3,2,1,0:T(8,128)} %param.26) | copy-start | bytes 294916
  6.6 26.4 %copy-start.4 = (s32[3,2,8,8]{3,2,1,0:T(8,128)S(1)}, s32[3,2,8,8]{3,2,1,0:T(8,128)}, u32[]{:S(2)}) copy-start(s32[3,2,8,8]{3,2,1,0:T(8,128)} %param.27) | copy-start | bytes 4612
  29.8 4.3 %copy-start.1 = (bf16[3,2,8,8,128]{4,3,2,1,0:T(8,128)(2,1)S(1)}, bf16[3,2,8,8,128]{4,3,2,1,0:T(8,128)(2,1)}, u32[]{:S(2)}) copy-start(bf16[3,2,8,8,128]{4,3,2,1,0:T(8,128)(2,1)} %param.23) | copy-start | bytes 294916
  29.8 4.3 %copy-start.3 = (bf16[128,128]{1,0:T(8,128)(2,1)S(1)}, bf16[128,128]{1,0:T(8,128)(2,1)}, u32[]{:S(2)}) copy-start(bf16[128,128]{1,0:T(8,128)(2,1)} %param.28) | copy-start | bytes 98308
  29.8 5.1 %copy-start.5 = (f32[8]{0:T(128)S(1)}, f32[8]{0:T(128)}, u32[]{:S(2)}) copy-start(f32[8]{0:T(128)} %param.31) | copy-start | bytes 100
where the time goes:
time: 98.3 us; the launch traced here: 97.4 us
  Pallas kernels  82.8 us (84%)
  other arithmetic  5.78 us (6%)
  local copies, waits for them, and re-layouts  5 us (5%)
  matrix products  3 us (3%)
    pallas_call x1, Pallas kernels, shards(): pl.pallas_call(functools.partial(pair_kernel, (cells_x, cells_y, cells_z)...  33.5 us
    pallas_call x1, Pallas kernels, shards(): pl.pallas_call(functools.partial(gather_kernel, sizes, cells), out_shape=...  22.4 us
    pallas_call x1, Pallas kernels, shards(): pl.pallas_call(functools.partial(charge_kernel, sizes, lengths, window, s...  14.3 us
    pallas_call x1, Pallas kernels, shards(): pl.pallas_call(functools.partial(scatter_kernel, sizes), out_shape=jax.Sh...  12.6 us
    reshape x1, other arithmetic, shards(): ext.astype(f32)  2.56 us

commit v1 on v0

--- a/solution.py
+++ b/solution.py
@@ -345,8 +345,51 @@
     return (gx * sizes[1] + gy) * sizes[2] + gz
 
 
-def gather_kernel(
-    sizes, cells, atoms_ref, rows_ref, all_ref, ext_ref, asend, arecv, hsend, hrecv, local_sem
+def fused_kernel(
+    sizes,
+    cells,
+    lengths,
+    window,
+    screen,
+    planes,
+    atoms_ref,
+    rows_ref,
+    code_ref,
+    own_ref,
+    hidden_ref,
+    wr_ref,
+    rates_ref,
+    w1_ref,
+    w2_ref,
+    wv_ref,
+    wo_ref,
+    zrow_ref,
+    krow_ref,
+    kx_ref,
+    by_ref,
+    byt_ref,
+    bx_ref,
+    bxt_ref,
+    out_ref,
+    site_ref,
+    all_ref,
+    near_ref,
+    ext_ref,
+    plane_ref,
+    wave_ref,
+    part_ref,
+    held_ref,
+    msg_ref,
+    vec_ref,
+    w1t_ref,
+    w2t_ref,
+    asend,
+    arecv,
+    hsend,
+    hrecv,
+    psend,
+    precv,
+    local_sem,
 ):
     devices = sizes[0] * sizes[1] * sizes[2]
     here = tuple(lax.axis_index(a) for a in AXES)
@@ -373,7 +416,7 @@
                 peer.append(lax.rem(here[axis] + sizes[axis] - 1, sizes[axis]))
         copy = pltpu.make_async_remote_copy(
             src_ref=rows_ref.at[tuple(source)],
-            dst_ref=ext_ref.at[tuple(target)],
+            dst_ref=near_ref.at[tuple(target)],
             send_sem=hsend.at[shift],
             recv_sem=hrecv.at[shift],
             device_id=tuple(peer),
@@ -381,11 +424,10 @@
         )
         copies.append(copy)
 
-    def atom_copy(o):
-        peer = lax.rem(me + o, devices)
+    def atom_copy(o, peer, slot):
         return pltpu.make_async_remote_copy(
             src_ref=atoms_ref,
-            dst_ref=all_ref.at[me],
+            dst_ref=all_ref.at[slot],
             send_sem=asend.at[o],
             recv_sem=arecv.at[o],
             device_id=coords_of(peer, sizes),
@@ -393,63 +435,105 @@
         )
 
     def start(o, carry):
-        atom_copy(o).start()
+        atom_copy(o, lax.rem(me + o, devices), me).start()
         return carry
 
     lax.fori_loop(1, devices, start, 0)
     for copy in copies:
         copy.start()
-    inner = tuple(pl.ds(1, size) for size in cells)
-    local = pltpu.make_async_copy(rows_ref, ext_ref.at[inner], local_sem.at[0])
-    local.start()
-    local_atoms = pltpu.make_async_copy(atoms_ref, all_ref.at[me], local_sem.at[1])
-    local_atoms.start()
-    local.wait()
-    local_atoms.wait()
+    all_ref[me] = atoms_ref[...]
 
     def finish(o, carry):
         origin = lax.rem(me + devices - o, devices)
-        pltpu.make_async_remote_copy(
-            src_ref=atoms_ref,
-            dst_ref=all_ref.at[origin],
-            send_sem=asend.at[o],
-            recv_sem=arecv.at[o],
-            device_id=coords_of(origin, sizes),
-            device_id_type=pl.DeviceIdType.MESH,
-        ).wait()
+        atom_copy(o, origin, origin).wait()
         return carry
 
     lax.fori_loop(1, devices, finish, 0)
-    for copy in copies:
-        copy.wait()
-
-
-def scatter_kernel(sizes, part_ref, out_ref, held_ref, send, recv):
-    devices = sizes[0] * sizes[1] * sizes[2]
-    me = my_index(sizes)
-
-    def copy_to(o):
-        peer = lax.rem(me + o, devices)
+    charge_kernel(
+        sizes,
+        lengths,
+        window,
+        screen,
+        planes,
+        all_ref,
+        zrow_ref,
+        krow_ref,
+        kx_ref,
+        by_ref,
+        byt_ref,
+        bx_ref,
+        bxt_ref,
+        part_ref,
+        plane_ref,
+        wave_ref,
+    )
+
+    def part_copy(o, peer):
         return pltpu.make_async_remote_copy(
             src_ref=part_ref.at[peer],
             dst_ref=held_ref.at[o],
-            send_sem=send.at[o],
-            recv_sem=recv.at[o],
+            send_sem=psend.at[o],
+            recv_sem=precv.at[o],
             device_id=coords_of(peer, sizes),
             device_id_type=pl.DeviceIdType.MESH,
         )
 
-    def start(o, carry):
-        copy_to(o).start()
+    def send(o, carry):
+        part_copy(o, lax.rem(me + o, devices)).start()
         return carry
 
-    lax.fori_loop(1, devices, start, 0)
-
-    def finish(o, total):
-        copy_to(o).wait()
+    lax.fori_loop(1, devices, send, 0)
+    for copy in copies:
+        copy.wait()
+    cells_x, cells_y, cells_z = cells
+    for x in range(cells_x + 2):
+        for y in range(cells_y + 2):
+            inside = 1 <= x <= cells_x and 1 <= y <= cells_y
+            column = x * (cells_y + 2) + y
+            if inside:
+                ext_ref[column, : slots_of(near_ref)] = flat32(near_ref[x, y, 0:1])
+                ext_ref[column, slots_of(near_ref) : -slots_of(near_ref)] = flat32(
+                    rows_ref[x - 1, y - 1]
+                )
+                ext_ref[column, -slots_of(near_ref) :] = flat32(
+                    near_ref[x, y, cells_z + 1 : cells_z + 2]
+                )
+            else:
+                ext_ref[column] = flat32(near_ref[x, y])
+    pair_kernel(
+        cells,
+        lengths,
+        code_ref,
+        ext_ref,
+        own_ref,
+        hidden_ref,
+        wr_ref,
+        rates_ref,
+        w1_ref,
+        w2_ref,
+        wv_ref,
+        wo_ref,
+        out_ref,
+        msg_ref,
+        vec_ref,
+        w1t_ref,
+        w2t_ref,
+    )
+
+    def take(o, total):
+        part_copy(o, lax.rem(me + o, devices)).wait()
         return total + held_ref[o]
 
-    out_ref[...] = lax.fori_loop(1, devices, finish, part_ref[me])
+    site_ref[...] = lax.fori_loop(1, devices, take, part_ref[me])
+
+
+def slots_of(ref):
+    return ref.shape[3]
+
+
+def flat32(block):
+    wide = block.astype(jnp.float32)
+    return wide.reshape(wide.shape[0] * wide.shape[1], wide.shape[2])
 
 
 def shards(
@@ -504,24 +588,6 @@
     cells = (cells_x, cells_y, cells_z)
     vmem = pl.BlockSpec(memory_space=pltpu.VMEM)
     dma = pltpu.SemaphoreType.DMA
-    atoms, ext = pl.pallas_call(
-        functools.partial(gather_kernel, sizes, cells),
-        out_shape=(
-            jax.ShapeDtypeStruct((devices,) + atoms.shape, f32),
-            jax.ShapeDtypeStruct(
-                tuple(c + 2 for c in cells) + (slot_count, 2 * channels), bf16
-            ),
-        ),
-        in_specs=[vmem] * 2,
-        out_specs=(vmem, vmem),
-        scratch_shapes=[dma((devices,)), dma((devices,)), dma((27,)), dma((27,)), dma((2,))],
-        name="gather_atoms",
-        compiler_params=pltpu.CompilerParams(has_side_effects=True),
-    )(atoms, rows)
-    ext = ext.astype(f32).reshape(
-        (cells_x + 2) * (cells_y + 2), (cells_z + 2) * slot_count, 2 * channels
-    )
-
     listed = neighbours.reshape(cells_x, cells_y, cells_z, slot_count * NBR)
     slot_ids = listed % slot_count
     cell_ids = listed // slot_count
@@ -537,37 +603,6 @@
     dead = jnp.arange(NBR, dtype=jnp.int32)[None, None, :] >= counts
     code = code.reshape(cell_count, slot_count, NBR) + jnp.where(dead, 256, 0)
     code = code.reshape(cell_count, 1, slot_count * NBR)
-
-    vmem = pl.BlockSpec(memory_space=pltpu.VMEM)
-    updated = pl.pallas_call(
-        functools.partial(pair_kernel, (cells_x, cells_y, cells_z), lengths),
-        out_shape=jax.ShapeDtypeStruct((atom_count, channels), bf16),
-        in_specs=[vmem] * 10,
-        out_specs=vmem,
-        scratch_shapes=[
-            pltpu.VMEM((atom_count, channels), f32),
-            pltpu.VMEM((3, atom_count, channels), f32),
-            pltpu.VMEM((channels, channels), bf16),
-            pltpu.VMEM((channels, channels), bf16),
-        ],
-        name="pair_layer",
-        cost_estimate=pl.CostEstimate(
-            flops=2 * atom_count * NBR * channels * 512,
-            bytes_accessed=4 * 1024 * 1024,
-            transcendentals=3 * atom_count * NBR * channels,
-        ),
-    )(
-        code,
-        ext,
-        own,
-        hidden,
-        w_radial,
-        radial_rates.reshape(-1, 1),
-        w_pair1,
-        w_pair2,
-        w_vector,
-        w_out,
-    )
 
     share = length_z // 2 // devices
     planes = 2 * share
@@ -600,21 +635,50 @@
     )
     by = basis_y[:, columns].astype(np.float32)
     bx = basis_x.astype(np.float32)
-    partial = pl.pallas_call(
-        functools.partial(charge_kernel, sizes, lengths, window, screen, planes),
-        out_shape=jax.ShapeDtypeStruct((devices, 1, atom_count), f32),
-        in_specs=[vmem] * 8,
-        out_specs=vmem,
+    updated, site_potential = pl.pallas_call(
+        functools.partial(fused_kernel, sizes, cells, lengths, window, screen, planes),
+        out_shape=(
+            jax.ShapeDtypeStruct((atom_count, channels), bf16),
+            jax.ShapeDtypeStruct((1, atom_count), f32),
+        ),
+        in_specs=[vmem] * 18,
+        out_specs=(vmem, vmem),
         scratch_shapes=[
+            pltpu.VMEM((devices,) + atoms.shape, f32),
+            pltpu.VMEM(tuple(c + 2 for c in cells) + (slot_count, 2 * channels), bf16),
+            pltpu.VMEM(
+                ((cells_x + 2) * (cells_y + 2), (cells_z + 2) * slot_count, 2 * channels), f32
+            ),
             pltpu.VMEM((planes, sizes[1] * window, length_x), f32),
             pltpu.VMEM((sizes[0] * sizes[1], planes, sizes[2] * atom_count), f32),
+            pltpu.VMEM((devices, 1, atom_count), f32),
+            pltpu.VMEM((devices, 1, atom_count), f32),
+            pltpu.VMEM((atom_count, channels), f32),
+            pltpu.VMEM((3, atom_count, channels), f32),
+            pltpu.VMEM((channels, channels), bf16),
+            pltpu.VMEM((channels, channels), bf16),
+            dma((devices,)),
+            dma((devices,)),
+            dma((27,)),
+            dma((27,)),
+            dma((devices,)),
+            dma((devices,)),
+            dma((2,)),
         ],
-        name="charge_solve",
-        cost_estimate=pl.CostEstimate(
-            flops=10**10, bytes_accessed=2 * 1024 * 1024, transcendentals=10**6
-        ),
+        name="fused_layer",
+        compiler_params=pltpu.CompilerParams(has_side_effects=True),
     )(
         atoms,
+        rows,
+        code,
+        own,
+        hidden,
+        w_radial,
+        radial_rates.reshape(-1, 1),
+        w_pair1,
+        w_pair2,
+        w_vector,
+        w_out,
         jnp.asarray(zrow),
         jnp.asarray(krow),
         jnp.asarray(kx),
@@ -623,19 +687,6 @@
         jnp.asarray(bx),
         jnp.asarray(np.ascontiguousarray(bx.T)),
     )
-    site_potential = pl.pallas_call(
-        functools.partial(scatter_kernel, sizes),
-        out_shape=jax.ShapeDtypeStruct((1, atom_count), f32),
-        in_specs=[vmem],
-        out_specs=vmem,
-        scratch_shapes=[
-            pltpu.VMEM((devices, 1, atom_count), f32),
-            dma((devices,)),
-            dma((devices,)),
-        ],
-        name="scatter_sum",
-        compiler_params=pltpu.CompilerParams(has_side_effects=True),
-    )(partial)
     return (
         updated.reshape(features.shape),
         site_potential.reshape(cells_x, cells_y, cells_z, slot_count),

time: 98.3 us -> 78.6 us (0.80)
  Pallas kernels: 82.8 us -> 64.8 us
  other arithmetic: 5.78 us -> 1.91 us
  local copies, waits for them, and re-layouts: 5 us -> 8.49 us
    pallas_call x4 -> x1, Pallas kernels: 82.8 us -> 64.8 us  [shards(): pl.pallas_call(functools.partial(fused_kernel, sizes, cells, lengths, win...]
    unnamed x13 -> x22, local copies, waits for them, and re-layouts: 0.88 us -> 4.37 us
    reshape x1 -> x0, other arithmetic: 2.56 us -> none  [shards(): ext.astype(f32)]
where the time goes in v1:
time: 78.6 us; the launch traced here: 78.1 us
  Pallas kernels  64.8 us (82%)
  local copies, waits for them, and re-layouts  8.49 us (11%)
  matrix products  2.12 us (3%)
  other arithmetic  1.91 us (2%)
  between operations  0.82 us (1%)
    pallas_call x1, Pallas kernels, shards(): pl.pallas_call(functools.partial(fused_kernel, sizes, cells, lengths, win...  64.8 us
    unnamed x22, local copies, waits for them, and re-layouts  4.37 us

profile of v1, /device:TPU:1, one launch (start us, length us, event | category | flops | bytes accessed | tf_op | source)
XLA Modules:
  0.0 78.1 jit_solution(9524666419250942396)
XLA Ops:
  0.7 0.8 %eq.22 = s32[384]{0:T(512)S(1)} reshape(s32[3,2,8,8]{3,2,1,0:T(8,128)} %param.25) | data formatting | bytes 3072 | tf_op jit(solution)/shard_map/eq | solution.py:574
  1.6 0.7 copy-done.7
  2.2 1.1 %convolution_reduce_fusion = f32[384]{0:T(512)S(1)} fusion(bf16[384,128]{1,0:T(8,128)(2,1)} %bitcast.23, bf16[128]{0:T(256)(128)(2,1)S(1)} %copy-done.7), kind=kOutput, calls=%fused_computation.1 | convolution fusion | flops 98304 | bytes 100096 | tf_op jit(solution)/shard_map/dot_general | solution.py:576
  3.3 0.1 copy.33
  3.5 0.1 reshape.83
  3.7 0.1 reshape.84
  3.8 0.6 pad_maximum_fusion.atoms_ref
  4.5 0.2 convolution_convert_fusion
  4.8 0.1 reshape.86
  4.9 0.1 concatenate.10
  5.1 0.8 %copy.36 = bf16[384,256]{1,0:T(8,128)(2,1)} copy(bf16[384,256]{0,1:T(8,128)(2,1)S(1)} %concatenate.10) | data formatting | bytes 393216 | tf_op jit(solution)/shard_map/concatenate | solution.py:586
  6.0 0.4 fusion.10
  6.4 0.1 reshape.88
  6.5 0.6 copy-done.4
  7.1 0.1 ge.32
  7.2 0.2 ge.33
  7.5 0.8 fusion.20.code_ref
  8.3 0.8 %fusion.27.own_ref = f32[384,128]{1,0:T(8,128)} fusion(bf16[384,128]{1,0:T(8,128)(2,1)S(1)} %bitcast.26, bf16[128,128]{1,0:T(8,128)(2,1)S(1)} %copy-done.3), kind=kOutput, calls=%fused_computation.61 | convolution fusion | flops 12582912 | bytes 327680 | tf_op jit(solution)/shard_map/dot_general | solution.py:569
  9.1 0.7 copy-done.9
  9.8 0.7 copy.37.rates_ref
  10.4 64.8 %fused_layer.1 = (bf16[384,128]{1,0:T(8,128)(2,1)}, f32[1,384]{1,0:T(1,128)}) custom-call(f32[4,384]{1,0:T(4,128)} %pad_maximum_fusion.atoms_ref, bf16[3,2,8,8,256]{4,3,2,1,0:T(8,128)(2,1)} %bitcast.27, s32[48,1,512]{2,1,0:T(1,128)} %fusion.20.code_ref, f32[384,128]{1,0:T(8,128)} %fusion.27.own_ref, bf16[384,128]{1,0:T(8,128)(2,1)} %bitcast.24, ...), custom_call_target="tpu_custom_call" | custom-call | tf_op jit(solution)/shard_map/fused_layer/pallas_call | solution.py:638
  75.2 0.6 copy-done.6
  75.9 0.7 reshape.91
  76.6 1.5 %copy.39 = bf16[3,2,8,8,128]{4,3,2,1,0:T(8,128)(2,1)} copy(bf16[3,2,8,8,128]{4,3,2,1,0:T(8,128)(2,1)} %bitcast.30) | data formatting | bytes 196608
  (27 shorter events, 0.6 us)
Async XLA Ops:
  0.6 3.7 %copy-start = (bf16[128,128]{1,0:T(8,128)(2,1)S(1)}, bf16[128,128]{1,0:T(8,128)(2,1)}, u32[]{:S(2)}) copy-start(bf16[128,128]{1,0:T(8,128)(2,1)} %param.29) | copy-start | bytes 98308
  0.6 0.8 %copy-start.8 = (f32[2]{0:T(128)S(1)}, f32[2]{0:T(128)}, u32[]{:S(2)}) copy-start(f32[2]{0:T(128)} %param.37) | copy-start | bytes 28
  1.6 0.7 copy-start.7
  2.2 1.1 %copy-start.5 = (f32[3,2,8,24]{3,2,1,0:T(8,128)S(1)}, f32[3,2,8,24]{3,2,1,0:T(8,128)}, u32[]{:S(2)}) copy-start(f32[3,2,8,24]{3,2,1,0:T(8,128)} %param.24) | copy-start | bytes 13828
  3.6 0.9 %copy-start.1 = (bf16[3,2,8,8,128]{4,3,2,1,0:T(8,128)(2,1)S(1)}, bf16[3,2,8,8,128]{4,3,2,1,0:T(8,128)(2,1)}, u32[]{:S(2)}) copy-start(bf16[3,2,8,8,128]{4,3,2,1,0:T(8,128)(2,1)} %param.23) | copy-start | bytes 294916
  5.1 0.9 %copy-start.2 = (s32[3,2,8,512]{3,2,1,0:T(8,128)S(1)}, s32[3,2,8,512]{3,2,1,0:T(8,128)}, u32[]{:S(2)}) copy-start(s32[3,2,8,512]{3,2,1,0:T(8,128)} %param.26) | copy-start | bytes 294916
  6.4 0.7 copy-start.4
  7.5 0.8 %copy-start.3 = (bf16[128,128]{1,0:T(8,128)(2,1)S(1)}, bf16[128,128]{1,0:T(8,128)(2,1)}, u32[]{:S(2)}) copy-start(bf16[128,128]{1,0:T(8,128)(2,1)} %param.28) | copy-start | bytes 98308
  9.1 0.7 copy-start.9
  75.2 0.6 copy-start.6

commit v2 on v1

v2 whole, which is shorter than its diff:
```python
import functools
import math

import jax
import jax.numpy as jnp
import numpy as np
from jax import lax
from jax.experimental import pallas as pl
from jax.experimental.pallas import tpu as pltpu
from jax.sharding import PartitionSpec as P

NBR = 64
CELL = 8
LANES = 128
STEP_CELLS = 8
FIRST_PART = 7
VMEM_BYTES = 60 * 1024 * 1024
AXES = ("gx", "gy", "gz")

coulomb_scale = 0.25
smearing = 1.0
f32, bf16, i32 = jnp.float32, jnp.bfloat16, jnp.int32


def coords_of(index, sizes):
    return (
        index // (sizes[1] * sizes[2]),
        (index // sizes[2]) % sizes[1],
        index % sizes[2],
    )


def index_of(coords, sizes):
    return (coords[0] * sizes[1] + coords[1]) * sizes[2] + coords[2]


def iota(shape, axis):
    return lax.broadcasted_iota(i32, shape, axis)


def split_by(value, size):
    if size & (size - 1) == 0:
        shift = size.bit_length() - 1
        return lax.shift_right_logical(value, shift), value & (size - 1)
    high = jnp.floor((value.astype(f32) + 0.5) * (1.0 / size)).astype(i32)
    return high, value - high * size


def two_pieces(x):
    hi = x.astype(bf16)
    return hi, (x - hi.astype(f32)).astype(bf16)


def mm(a, b):
    return jnp.dot(a, b, preferred_element_type=f32)


def mm_nt(a, b):
    return lax.dot_general(a, b, (((1,), (1,)), ((), ())), preferred_element_type=f32)


def lane_pick(table, index):
    return jnp.take_along_axis(table, index, axis=1)


def silu_of_half(half):
    return (half + half * jnp.tanh(half)).astype(bf16)


def trig_basis(length):
    r = np.arange(length)
    rows = [np.cos(2 * np.pi * ((k * r) % length) / length) for k in range(length // 2 + 1)]
    rows += [np.sin(2 * np.pi * ((k * r) % length) / length) for k in range(1, length // 2)]
    modes = np.array(list(range(length // 2 + 1)) + list(range(1, length // 2)))
    return np.stack(rows), modes


def axis_terms(modes, length):
    wave = modes * (2.0 * np.pi / length)
    turn = np.exp(2j * np.pi * modes / length)
    modulus = np.abs(1 / 6 + 4 / 6 * turn + 1 / 6 * turn * turn) ** 2
    weight = np.where((modes == 0) | (2 * modes == length), 1.0, 2.0) / length
    return wave * wave, weight / modulus


def host_pieces(table):
    table = np.ascontiguousarray(table).astype(np.float32)
    hi = table.astype(jnp.bfloat16)
    lo = (table - hi.astype(np.float32)).astype(jnp.bfloat16)
    return jnp.asarray(hi), jnp.asarray(lo)


def layer_kernel(
    sizes,
    cells,
    lengths,
    screen,
    planes,
    win_x,
    win_y,
    feat_ref,
    hidden_ref,
    pos_ref,
    kind_ref,
    nbr_ref,
    count_ref,
    ws_ref,
    wn_ref,
    wr_ref,
    rates_ref,
    w1_ref,
    w2_ref,
    wv_ref,
    wo_ref,
    wc_ref,
    kinds_ref,
    zrow_ref,
    krow_ref,
    kx_ref,
    by_h_ref,
    by_l_ref,
    byt_h_ref,
    byt_l_ref,
    bxt_h_ref,
    bxt_l_ref,
    bxq_h_ref,
    bxq_l_ref,
    out_ref,
    site_ref,
    atoms_ref,
    all_ref,
    near_ref,
    sent_ref,
    own_ref,
    which_ref,
    zlane_ref,
    column_ref,
    live_ref,
    green_ref,
    line_ref,
    mine_ref,
    basis_ref,
    reach_ref,
    ztab_ref,
    plane_ref,
    along_ref,
    field_ref,
    wave_ref,
    xs_ref,
    ys_ref,
    part_ref,
    held_ref,
    msg_ref,
    vec_ref,
    bd1_ref,
    bd2_ref,
    asend,
    arecv,
    hsend,
    hrecv,
    psend,
    precv,
):
    size_x, size_y, size_z = sizes
    cells_x, cells_y, cells_z = cells
    length_x, length_y, length_z = lengths
    devices = size_x * size_y * size_z
    slots = feat_ref.shape[3]
    channels = feat_ref.shape[4]
    cell_count = cells_x * cells_y * cells_z
    atom_count = cell_count * slots
    pairs = slots * NBR
    half_pairs = pairs // 2
    run = cells_z * slots
    wide_y = cells_y + 2
    here = tuple(lax.axis_index(a) for a in AXES)
    me = index_of(here, sizes)

    offsets = [
        (a, b, c)
        for a in range(size_x)
        for b in range(size_y)
        for c in range(size_z)
        if (a, b, c) != (0, 0, 0)
    ]
    close = [
        all(step in (0, 1, size - 1) for step, size in zip(offset, sizes)) for offset in offsets
    ]
    offsets = [o for o, c in zip(offsets, close) if c] + [o for o, c in zip(offsets, close) if not c]
    close_count = sum(close)

    def moved(offset, sign):
        return tuple(
            lax.rem(at + (step if sign > 0 else size - step), size) if step else at
            for at, step, size in zip(here, offset, sizes)
        )

    barrier = pltpu.get_barrier_semaphore()
    for offset in offsets:
        pl.semaphore_signal(
            barrier, inc=1, device_id=moved(offset, 1), device_id_type=pl.DeviceIdType.MESH
        )

    pad_rows = jnp.zeros((LANES - cell_count, 1), f32)
    kinds = kind_ref[...].astype(f32)
    turned = [
        jnp.concatenate(
            [block, jnp.zeros((LANES - cell_count, block.shape[1]), f32)], axis=0
        ).T
        for block in (pos_ref[...], kinds)
    ]
    lane8 = iota((slots, LANES), 1)
    diagonal = (lane8 % slots) == iota((slots, LANES), 0)
    per_chunk = LANES // slots
    wc_rows = jnp.broadcast_to(wc_ref[...].reshape(1, channels), (slots, channels))
    readout = mm_nt(wc_rows, hidden_ref[...])

    def lined(block, chunk):
        picked = lane_pick(block, lane8 // slots + chunk * per_chunk)
        return jnp.sum(jnp.where(diagonal, picked, 0.0), axis=0, keepdims=True)

    for chunk in range(atom_count // LANES):
        where_to = slice(chunk * LANES, (chunk + 1) * LANES)
        for d in range(3):
            atoms_ref[d : d + 1, where_to] = lined(turned[0][d * slots : (d + 1) * slots], chunk)
        kind = lined(turned[1], chunk)
        charge = readout[0:1, where_to]
        for k in range(kinds_ref.shape[0]):
            charge = charge + jnp.where(kind == float(k), kinds_ref[k], 0.0)
        atoms_ref[3:4, where_to] = charge

    def atom_copy(offset, peer, slot):
        at = index_of(offset, sizes)
        return pltpu.make_async_remote_copy(
            src_ref=atoms_ref,
            dst_ref=all_ref.at[slot],
            send_sem=asend.at[at],
            recv_sem=arecv.at[at],
            device_id=peer,
            device_id_type=pl.DeviceIdType.MESH,
        )

    def wait_atoms(some):
        for offset in some:
            origin = moved(offset, -1)
            atom_copy(offset, origin, index_of(origin, sizes)).wait()

    copies = []
    for shift in range(27):
        step = (shift // 9 - 1, shift // 3 % 3 - 1, shift % 3 - 1)
        if step == (0, 0, 0):
            continue
        source, target, peer = [], [], []
        for axis in range(3):
            size = cells[axis]
            if step[axis] == 0:
                source.append(pl.ds(0, size))
                target.append(pl.ds(1, size))
                peer.append(here[axis])
            elif step[axis] > 0:
                source.append(pl.ds(size - 1, 1))
                target.append(pl.ds(0, 1))
                peer.append(lax.rem(here[axis] + 1, sizes[axis]))
            else:
                source.append(pl.ds(0, 1))
                target.append(pl.ds(size + 1, 1))
                peer.append(lax.rem(here[axis] + sizes[axis] - 1, sizes[axis]))
        copies.append(
            pltpu.make_async_remote_copy(
                src_ref=feat_ref.at[tuple(source)],
                dst_ref=near_ref.at[tuple(target)],
                send_sem=hsend.at[shift],
                recv_sem=hrecv.at[shift],
                device_id=tuple(peer),
                device_id_type=pl.DeviceIdType.MESH,
            )
        )
    pl.semaphore_wait(barrier, devices - 1)
    for offset in offsets[:close_count]:
        atom_copy(offset, moved(offset, 1), me).start()
    for copy in copies:
        copy.start()
    for offset in offsets[close_count:]:
        atom_copy(offset, moved(offset, 1), me).start()
    all_ref[me] = atoms_ref[...]

    own = mm(hidden_ref[...], ws_ref[...]) * 0.5
    own_hi = own.astype(bf16).astype(f32)
    own_ref[0] = own_hi
    own_ref[1] = (own - own_hi).astype(bf16).astype(f32)

    no_block = jnp.zeros((channels, channels), bf16)
    for ref, target in ((w1_ref, bd1_ref), (w2_ref, bd2_ref)):
        weight = ref[...] * jnp.asarray(0.5, bf16)
        target[0:channels, 0:channels] = weight
        target[0:channels, channels:] = no_block
        target[channels:, 0:channels] = no_block
        target[channels:, channels:] = weight

    listed = nbr_ref[...]
    cell_id, slot_id = split_by(listed, slots)
    xy_id, z_id = split_by(cell_id, cells_z * size_z)
    x_id, y_id = split_by(xy_id, cells_y * size_y)
    row_xy, row_z = split_by(iota((cell_count, 1), 0), cells_z)
    row_x, row_y = split_by(row_xy, cells_y)
    steps = []
    for ids, local, axis in ((x_id, row_x, 0), (y_id, row_y, 1), (z_id, row_z, 2)):
        total = cells[axis] * sizes[axis]
        gap = ids - (local + here[axis] * cells[axis])
        gap = jnp.where(gap > 1, gap - total, gap)
        steps.append(jnp.where(gap < -1, gap + total, gap))
    which = ((steps[0] + 1) * 3 + steps[1] + 1) * (3 * slots) + (steps[2] + 1) * slots + slot_id
    which_ref[...] = which.astype(f32)
    zlane_ref[...] = ((row_z + steps[2]) * slots + slot_id) & (LANES - 1)
    column_ref[...] = (steps[0] + 1) * wide_y + row_y + 1 + steps[1]
    lane_pair = iota((slots, pairs), 1)
    sel = jnp.where(lane_pair // NBR == iota((slots, pairs), 0), 1.0, 0.0)
    limit = mm(count_ref[...].astype(f32).astype(bf16), sel.astype(bf16))
    order = (iota((1, pairs), 1) % NBR).astype(f32)
    live_ref[...] = jnp.where(order < limit, 1.0, 0.0)

    zrow = zrow_ref[me]
    kcol = krow_ref[...]
    for j in range(planes):
        q = kcol[:, 0:1] + zrow[j : j + 1, 3:4] + kx_ref[0:1, :]
        scale = kcol[:, 1:2] * zrow[j : j + 1, 4:5] * kx_ref[1:2, :]
        green = (coulomb_scale * 4.0 * math.pi) * jnp.exp(-0.5 * smearing * smearing * q)
        green = green * scale / (q + 1.0 / (screen * screen))
        green_ref[j * length_y : (j + 1) * length_y] = jnp.where(q == 0.0, 0.0, green)
    plane_ref[...] = jnp.zeros(plane_ref.shape, f32)
    for z in range(size_z):
        lane = (iota((1, LANES), 1) + (z * cells_z * CELL - 1)).astype(f32)
        turns = zrow[:, 0:1] * lane
        turns = turns - length_z * jnp.floor(turns * (1.0 / length_z))
        angle = (turns - 0.5 * length_z) * (2.0 * math.pi / length_z)
        ztab_ref[z] = -jnp.cos(angle) * zrow[:, 1:2] - jnp.sin(angle) * zrow[:, 2:3]

    wait_atoms(offsets[:close_count])

    lane4 = iota((4, LANES), 1)
    for x in range(cells_x + 2):
        for pair_y in range(wide_y // 2):
            halves = []
            for y in (2 * pair_y, 2 * pair_y + 1):
                spots, locals_ = [], []
                for at, axis in ((x, 0), (y, 1)):
                    size = cells[axis]
                    if at == 0:
                        spots.append(lax.rem(here[axis] + sizes[axis] - 1, sizes[axis]))
                        locals_.append(size - 1)
                    elif at == size + 1:
                        spots.append(lax.rem(here[axis] + 1, sizes[axis]))
                        locals_.append(0)
                    else:
                        spots.append(here[axis])
                        locals_.append(at - 1)
                column = locals_[0] * cells_y + locals_[1]
                start_lane = column * run
                block = pl.ds(start_lane // LANES * LANES, LANES)
                odd = start_lane % LANES != 0
                pieces = []
                for step_z in (0, 1, size_z - 1):
                    origin = index_of(
                        (spots[0], spots[1], lax.rem(here[2] + step_z, size_z)), sizes
                    )
                    piece = all_ref[origin, :, block]
                    if (step_z == 0) == odd:
                        piece = pltpu.roll(piece, run, 1)
                    pieces.append(piece)
                line = jnp.where(
                    lane4 < run, pieces[0], jnp.where(lane4 < run + slots, pieces[1], pieces[2])
                )
                halves.append(line)
                if 1 <= x <= cells_x and 1 <= y <= cells_y:
                    mine_ref[column] = jnp.concatenate([line, line], axis=0)
            line_ref[x * (wide_y // 2) + pair_y] = jnp.concatenate(halves, axis=0)

    sub8 = iota((slots, LANES), 0)
    row_d = iota((slots, 1), 0)
    box = jnp.where(
        row_d == 0,
        float(length_x),
        jnp.where(row_d == 1, float(length_y), float(length_z)),
    )
    box_inv = 1.0 / box
    rates = jnp.zeros((rates_ref.shape[0], 1), f32)
    for k in range(rates_ref.shape[0]):
        rates = jnp.where(iota(rates.shape, 0) == k, rates_ref[k], rates)
    sub_y = sub8 // 4

    def geometry(octet, carry):
        rows = pl.ds(pl.multiple_of(octet * 8, 8), 8)
        for r in range(8):
            place_cell(octet * 8 + r, rows, r)
        return carry

    def place_cell(c, rows, r):
        cz = lax.rem(c, cells_z)
        cxy = c // cells_z
        cx = cxy // cells_y
        for chunk in range(pairs // LANES):
            part = pl.ds(chunk * LANES, LANES)
            spot = jnp.broadcast_to(zlane_ref[rows, part][r : r + 1], (slots, LANES))
            column = jnp.broadcast_to(column_ref[rows, part][r : r + 1], (slots, LANES)) - sub_y
            live = live_ref[rows, part][r : r + 1]
            which = which_ref[rows, part][r : r + 1]
            found = jnp.zeros((slots, LANES), f32)
            for dx in range(3):
                for pair_y in range(wide_y // 2):
                    table = line_ref[(cx + dx) * (wide_y // 2) + pair_y]
                    picked = lane_pick(table, spot)
                    found = jnp.where(column == dx * wide_y + 2 * pair_y, picked, found)
            found = found + pltpu.roll(found, 4, 0)
            own_spot = cz * slots + (lane8 + chunk * LANES) // NBR
            displace = found - lane_pick(mine_ref[cxy], own_spot)
            displace = displace - box * jnp.floor(displace * box_inv + 0.5)
            scaled = jnp.where(row_d < 3, displace * (1.0 / CELL), 0.0)
            square = jnp.sum(scaled * scaled, axis=0, keepdims=True)
            basis_ref[c, :, part] = jnp.exp(-square * rates)
            reach = jnp.where(row_d == 3, 1.0, scaled) * live
            reach_ref[c, :, part] = jnp.where(row_d == 4, which, reach)

    lax.fori_loop(0, cell_count // 8, geometry, 0)

    for copy in copies:
        copy.wait()
    for x in range(cells_x + 2):
        for y in range(wide_y):
            if 1 <= x <= cells_x and 1 <= y <= cells_y:
                blocks = [
                    near_ref[x, y, 0:1],
                    feat_ref[x - 1, y - 1],
                    near_ref[x, y, cells_z + 1 :],
                ]
            else:
                blocks = [near_ref[x, y]]
            line = [b.astype(f32).reshape(b.shape[0] * slots, channels) for b in blocks]
            line = jnp.concatenate(line, axis=0).astype(bf16)
            sent_ref[x * wide_y + y] = mm(line, wn_ref[...]).astype(bf16).astype(f32) * 0.5

    hot_rows = 27 * slots
    even_rows = hot_rows // 16 * 16
    hot_ids = iota((even_rows, 1), 0).astype(f32).astype(bf16)
    last_ids = (iota((hot_rows - even_rows, 1), 0) + even_rows).astype(f32)
    wr_rows = wr_ref[...].astype(f32) * 0.5
    sel_tile = jnp.concatenate([sel, sel], axis=0).astype(bf16)
    sub_h = iota((slots, half_pairs), 0)
    slot_h = iota((slots, half_pairs), 1) // NBR
    in_low = slot_h == sub_h
    in_high = slot_h == sub_h - slots // 2

    def pair_step(step, carry):
        rows = []
        for u in range(STEP_CELLS):
            c = step * STEP_CELLS + u
            cz = lax.rem(c, cells_z)
            cxy = c // cells_z
            cy = lax.rem(cxy, cells_y)
            cx = cxy // cells_y
            at = pl.ds(pl.multiple_of(cz * slots, slots), 3 * slots)
            mine = pl.ds(pl.multiple_of(c * slots, slots), slots)
            parts = []
            for dx in range(3):
                for dy in range(3):
                    parts.append(sent_ref[(cx + dx) * wide_y + cy + dy, at, :])
            parts += [wr_rows, own_ref[0, mine, :], own_ref[1, mine, :]]
            table = jnp.concatenate(parts, axis=0).astype(bf16).T
            which = reach_ref[c, 4:5, :]
            hot = jnp.where(
                hot_ids == which.astype(bf16), jnp.asarray(1.0, bf16), jnp.asarray(0.0, bf16)
            )
            last = jnp.where(last_ids == which, 1.0, 0.0)
            tile = jnp.concatenate([last, basis_ref[c]], axis=0).astype(bf16)
            rhs = jnp.concatenate([hot, tile, sel_tile], axis=0)
            latent = silu_of_half(mm(table, rhs)).T
            rows.append(jnp.concatenate([latent[:half_pairs], latent[half_pairs:]], axis=1))
        second = silu_of_half(mm(jnp.concatenate(rows, axis=0), bd1_ref[...]))
        third = silu_of_half(mm(second, bd2_ref[...]))
        for u in range(STEP_CELLS):
            c = step * STEP_CELLS + u
            mine = pl.ds(pl.multiple_of(c * slots, slots), slots)
            weights = []
            for r in (3, 0, 1, 2):
                low = reach_ref[c, r : r + 1, 0:half_pairs]
                high = reach_ref[c, r : r + 1, half_pairs:]
                full = jnp.where(in_low, low, jnp.where(in_high, high, 0.0))
                if r == 3:
                    weights.append(full)
                else:
                    full_hi = full.astype(bf16).astype(f32)
                    weights += [full_hi, full - full_hi]
            weights = jnp.concatenate(weights, axis=0).astype(bf16)
            sums = mm(weights, third[u * half_pairs : (u + 1) * half_pairs])
            rest = []
            for r in range(7):
                block = sums[r * slots : (r + 1) * slots]
                rest.append(
                    jnp.where(row_d < slots // 2, block[:, :channels], block[:, channels:])
                )
            msg_ref[mine, :] = rest[0] * (1.0 / NBR)
            for d in range(3):
                vec_ref[d, mine, :] = rest[1 + 2 * d] + rest[2 + 2 * d]
        return carry

    first_steps = cell_count // STEP_CELLS * FIRST_PART // 16
    lax.fori_loop(0, first_steps, pair_step, 0)
    wait_atoms(offsets[close_count:])

    lanes = size_z * atom_count

    def spread(g, carry):
        gx = g // size_y
        gy = lax.rem(g, size_y)
        base = g * size_z
        atoms = jnp.concatenate([all_ref[base + i] for i in range(size_z)], axis=1)
        whole = jnp.floor(atoms)
        f = atoms - whole
        sq = f * f
        cube = sq * f
        rem = 1.0 - f
        taps = [
            rem * rem * rem * (1.0 / 6.0),
            (3.0 * cube - 6.0 * sq + 4.0) * (1.0 / 6.0),
            (-3.0 * cube + 3.0 * sq + 3.0 * f + 1.0) * (1.0 / 6.0),
            cube * (1.0 / 6.0),
        ]
        first_x = (gx * (cells_x * CELL)).astype(f32)
        first_y = (gy * (cells_y * CELL)).astype(f32)
        off_x = iota((win_x, 1), 0).astype(f32).astype(bf16) - (whole[0:1] - first_x).astype(bf16)
        x_hi = jnp.zeros((win_x, lanes), bf16)
        x_lo = jnp.zeros((win_x, lanes), bf16)
        for t in range(4):
            hit = off_x == jnp.asarray(t, bf16)
            t_hi, t_lo = two_pieces(taps[t][0:1])
            x_hi = jnp.where(hit, jnp.broadcast_to(t_hi, hit.shape), x_hi)
            x_lo = jnp.where(hit, jnp.broadcast_to(t_lo, hit.shape), x_lo)
        off_y = iota((win_y, 1), 0).astype(f32) - (whole[1:2] - first_y)
        rows_y = jnp.zeros((win_y, lanes), f32)
        for t in range(4):
            rows_y = jnp.where(off_y == float(t), taps[t][1:2], rows_y)
        waves = []
        for z in range(size_z):
            table = ztab_ref[z]
            for chunk in range(atom_count // LANES):
                part = slice(z * atom_count + chunk * LANES, z * atom_count + (chunk + 1) * LANES)
                spot = (whole[2:3, part] - float(z * cells_z * CELL)).astype(i32)
                spot = jnp.broadcast_to(spot, table.shape)
                wave = None
                for t in range(4):
                    term = lane_pick(table, spot + t) * taps[t][2:3, part]
                    wave = term if wave is None else wave + term
                waves.append(wave)
        wave = jnp.concatenate(waves, axis=1)
        wave_ref[g] = wave
        ys_ref[g] = rows_y
        rows_x = jnp.concatenate([x_hi, x_lo], axis=0)
        xs_ref[g] = rows_x
        scaled = wave * atoms[3:4]
        left = jnp.concatenate([rows_y * scaled[j : j + 1] for j in range(planes)], axis=0)
        l_hi, l_lo = two_pieces(left)
        res = mm_nt(l_hi, rows_x) + mm_nt(l_lo, rows_x)
        per_block = LANES // (2 * win_x)
        res = jnp.concatenate([res, jnp.zeros((res.shape[0], LANES - 2 * win_x), f32)], axis=1)
        res = pltpu.roll(res, lax.rem(gx, per_block) * (2 * win_x), 1)
        rows = pl.ds(pl.multiple_of(gy * win_y, 8), win_y)
        for j in range(planes):
            plane_ref[gx // per_block, j, rows, :] += res[j * win_y : (j + 1) * win_y]
        return carry

    lax.fori_loop(0, size_x * size_y, spread, 0)

    spectrum = None
    for block in range(plane_ref.shape[0]):
        for j in range(planes):
            p_hi, p_lo = two_pieces(plane_ref[block, j])
            along_ref[j * length_y : (j + 1) * length_y, :] = (
                mm(by_h_ref[...], p_hi) + mm(by_h_ref[...], p_lo) + mm(by_l_ref[...], p_hi)
            )
        a_hi, a_lo = two_pieces(along_ref[...])
        part = mm(a_hi, bxt_h_ref[block]) + mm(a_lo, bxt_h_ref[block]) + mm(a_hi, bxt_l_ref[block])
        spectrum = part if spectrum is None else spectrum + part
    s_hi, s_lo = two_pieces(spectrum * green_ref[...])
    lane_x = iota((1, LANES), 1) % (2 * win_x) < win_x
    for gx in range(size_x):
        cols = slice(gx * LANES, (gx + 1) * LANES)
        back = mm(s_hi, bxq_h_ref[:, cols]) + mm(s_lo, bxq_h_ref[:, cols]) + mm(s_hi, bxq_l_ref[:, cols])
        b_hi, b_lo = two_pieces(back)
        for j in range(planes):
            rows = slice(j * length_y, (j + 1) * length_y)
            value = (
                mm(byt_h_ref[...], b_hi[rows])
                + mm(byt_h_ref[...], b_lo[rows])
                + mm(byt_l_ref[...], b_hi[rows])
            )
            v_hi = value.astype(bf16).astype(f32)
            field_ref[gx, j] = jnp.where(lane_x, v_hi, value - v_hi)

    def part_copy(o, peer):
        return pltpu.make_async_remote_copy(
            src_ref=part_ref.at[peer],
            dst_ref=held_ref.at[o],
            send_sem=psend.at[o],
            recv_sem=precv.at[o],
            device_id=coords_of(peer, sizes),
            device_id_type=pl.DeviceIdType.MESH,
        )

    def sample(g, carry):
        gx = g // size_y
        gy = lax.rem(g, size_y)
        rows = pl.ds(pl.multiple_of(gy * win_y, 8), win_y)
        field = jnp.concatenate([field_ref[gx, j, rows, :] for j in range(planes)], axis=0)
        x_hi = xs_ref[g, 0:win_x]
        x_lo = xs_ref[g, win_x:]
        stack = [x_hi, x_hi, x_lo, x_lo] + [jnp.zeros_like(x_hi)] * (LANES // win_x - 4)
        values = mm(field.astype(bf16), jnp.concatenate(stack, axis=0))
        wave = wave_ref[g]
        mixed = values[0:win_y] * wave[0:1]
        for j in range(1, planes):
            mixed = mixed + values[j * win_y : (j + 1) * win_y] * wave[j : j + 1]
        line = jnp.sum(mixed * ys_ref[g], axis=0, keepdims=True)
        for i in range(size_z):
            part_ref[g * size_z + i] = line[:, i * atom_count : (i + 1) * atom_count]
        return carry

    lax.fori_loop(0, size_x * size_y, sample, 0)

    def send(o, carry):
        part_copy(o, lax.rem(me + o, devices)).start()
        return carry

    lax.fori_loop(1, devices, send, 0)

    lax.fori_loop(first_steps, cell_count // STEP_CELLS, pair_step, 0)

    invariant = None
    for d in range(3):
        v_hi, v_lo = two_pieces(vec_ref[d])
        vector = (mm(v_hi, wv_ref[...]) + mm(v_lo, wv_ref[...])) * (1.0 / math.sqrt(NBR))
        part = vector * vector
        invariant = part if invariant is None else invariant + part
    update = (msg_ref[...] + invariant).astype(bf16)
    out_ref[...] = (hidden_ref[...].astype(f32) + mm(update, wo_ref[...])).astype(bf16)

    def take(o, total):
        part_copy(o, lax.rem(me + o, devices)).wait()
        return total + held_ref[o]

    total = lax.fori_loop(1, devices, take, part_ref[me])
    rows = LANES // slots
    spot = iota((rows, LANES), 0) * slots + lax.rem(iota((rows, LANES), 1), slots)
    for chunk in range(atom_count // LANES):
        line = jnp.broadcast_to(total[:, chunk * LANES : (chunk + 1) * LANES], (rows, LANES))
        site_ref[chunk * rows : (chunk + 1) * rows, :] = lane_pick(line, spot)[:, :slots]


def shards(
    features,
    positions,
    grid_anchor,
    species,
    neighbours,
    neighbour_count,
    w_self,
    w_neighbour,
    w_radial,
    radial_rates,
    w_pair1,
    w_pair2,
    w_vector,
    w_out,
    w_charge,
    species_charge,
):
    cells_x, cells_y, cells_z, slot_count, channels = features.shape
    cells = (cells_x, cells_y, cells_z)
    cell_count = cells_x * cells_y * cells_z
    atom_count = cell_count * slot_count
    sizes = tuple(lax.axis_size(a) for a in AXES)
    devices = sizes[0] * sizes[1] * sizes[2]
    lengths = tuple(c * s * CELL for c, s in zip(cells, sizes))
    length_x, length_y, length_z = lengths
    screen = 2 * cells_y * CELL
    pairs = slot_count * NBR

    share = length_z // 2 // devices
    planes = 2 * share
    win_x = -(-(cells_x * CELL + 4) // 8) * 8
    win_y = -(-(cells_y * CELL + 4) // 8) * 8
    assert 2 * cells_z * slot_count == LANES and cells_y % 2 == 0
    assert LANES % (4 * win_x) == 0 and cells_z * CELL + 4 <= LANES
    all_modes = np.arange(length_z // 2)
    table_k = np.stack([all_modes, all_modes], axis=1)
    phase_c = np.stack([np.ones_like(all_modes), np.zeros_like(all_modes)], axis=1)
    table_k[0, 1] = length_z // 2
    phase_c[0, 1] = 1
    table_k = table_k.reshape(devices, planes)
    phase_c = phase_c.reshape(devices, planes).astype(np.float64)
    basis_x, modes_x = trig_basis(length_x)
    basis_y, modes_y = trig_basis(length_y)
    qx, sx = axis_terms(modes_x, length_x)
    qy, sy = axis_terms(modes_y, length_y)
    qz, sz = axis_terms(table_k, length_z)
    krow = np.stack([qy, sy], axis=1).astype(np.float32)
    zrow = np.stack([table_k, phase_c, 1.0 - phase_c, qz, sz], axis=2)
    plane_rows = -(-planes // 8) * 8
    zrow = np.concatenate([zrow, np.ones((devices, plane_rows - planes, 5))], axis=1)
    zrow = zrow.astype(np.float32)
    kx = np.stack([qx, sx]).astype(np.float32)
    grid_x, grid_y = cells_x * CELL, cells_y * CELL
    at_y = np.concatenate([(np.arange(win_y) + g * grid_y - 1) % length_y for g in range(sizes[1])])
    by = basis_y[:, at_y]
    per_block = LANES // (2 * win_x)
    blocks = -(-sizes[0] // per_block)
    forward = np.zeros((blocks, LANES, length_x))
    backward = np.zeros((length_x, sizes[0] * LANES))
    for g in range(sizes[0]):
        cols = basis_x[:, (np.arange(win_x) + g * grid_x - 1) % length_x]
        at = g % per_block * 2 * win_x
        forward[g // per_block, at : at + 2 * win_x] = np.concatenate([cols, cols], axis=1).T
        backward[:, g * LANES : g * LANES + 4 * win_x] = np.concatenate([cols] * 4, axis=1)
    tables = [jnp.asarray(zrow), jnp.asarray(krow), jnp.asarray(kx)]
    for table in (by, by.T, forward, backward):
        tables += host_pieces(table)

    vmem = pl.BlockSpec(memory_space=pltpu.VMEM)
    smem = pl.BlockSpec(memory_space=pltpu.SMEM)
    dma = pltpu.SemaphoreType.DMA
    groups = sizes[0] * sizes[1]
    lanes = sizes[2] * atom_count
    columns = (cells_x + 2) * (cells_y + 2)
    updated, site_potential = pl.pallas_call(
        functools.partial(layer_kernel, sizes, cells, lengths, screen, planes, win_x, win_y),
        out_shape=(
            jax.ShapeDtypeStruct((atom_count, channels), bf16),
            jax.ShapeDtypeStruct((cell_count, slot_count), f32),
        ),
        in_specs=[vmem] * 9 + [smem] + [vmem] * 5 + [smem] + [vmem] * 11,
        out_specs=(vmem, vmem),
        scratch_shapes=[
            pltpu.VMEM((4, atom_count), f32),
            pltpu.VMEM((devices, 4, atom_count), f32),
            pltpu.VMEM(tuple(c + 2 for c in cells) + (slot_count, channels), bf16),
            pltpu.VMEM((columns, (cells_z + 2) * slot_count, channels), f32),
            pltpu.VMEM((2, atom_count, channels), f32),
            pltpu.VMEM((cell_count, pairs), f32),
            pltpu.VMEM((cell_count, pairs), i32),
            pltpu.VMEM((cell_count, pairs), i32),
            pltpu.VMEM((cell_count, pairs), f32),
            pltpu.VMEM((planes * length_y, length_x), f32),
            pltpu.VMEM((columns // 2, 8, LANES), f32),
            pltpu.VMEM((cells_x * cells_y, 8, LANES), f32),
            pltpu.VMEM((cell_count, 8, pairs), f32),
            pltpu.VMEM((cell_count, 8, pairs), f32),
            pltpu.VMEM((sizes[2], plane_rows, LANES), f32),
            pltpu.VMEM((blocks, planes, sizes[1] * win_y, LANES), f32),
            pltpu.VMEM((planes * length_y, LANES), f32),
            pltpu.VMEM((sizes[0], planes, sizes[1] * win_y, LANES), f32),
            pltpu.VMEM((groups, plane_rows, lanes), f32),
            pltpu.VMEM((groups, 2 * win_x, lanes), bf16),
            pltpu.VMEM((groups, win_y, lanes), f32),
            pltpu.VMEM((devices, 1, atom_count), f32),
            pltpu.VMEM((devices, 1, atom_count), f32),
            pltpu.VMEM((atom_count, channels), f32),
            pltpu.VMEM((3, atom_count, channels), f32),
            pltpu.VMEM((2 * channels, 2 * channels), bf16),
            pltpu.VMEM((2 * channels, 2 * channels), bf16),
            dma((devices,)),
            dma((devices,)),
            dma((27,)),
            dma((27,)),
            dma((devices,)),
            dma((devices,)),
        ],
        name="fused_layer",
        compiler_params=pltpu.CompilerParams(
            has_side_effects=True, collective_id=0, vmem_limit_bytes=VMEM_BYTES
        ),
    )(
        features,
        features.reshape(atom_count, channels),
        positions.reshape(cell_count, 3 * slot_count),
        species.reshape(cell_count, slot_count),
        neighbours.reshape(cell_count, pairs),
        neighbour_count.reshape(cell_count, slot_count),
        w_self,
        w_neighbour,
        w_radial,
        radial_rates,
        w_pair1,
        w_pair2,
        w_vector,
        w_out,
        w_charge,
        species_charge,
        *tables,
    )
    return (
        updated.reshape(features.shape),
        site_potential.reshape(cells_x, cells_y, cells_z, slot_count),
    )


def solution(mesh):
    cells = P("gx", "gy", "gz", None)
    return jax.shard_map(
        shards,
        mesh=mesh,
        in_specs=(P("gx", "gy", "gz", None, None),) + (cells,) * 5 + (P(),) * 10,
        out_specs=(P("gx", "gy", "gz", None, None), cells),
        check_vma=False,
    )
```

time: 78.6 us -> 40.6 us (0.52)
  Pallas kernels: 64.8 us -> 37.6 us
  local copies, waits for them, and re-layouts: 8.49 us -> 2.16 us
  matrix products: 2.12 us -> 0 us
  other arithmetic: 1.91 us -> 0 us
    pallas_call x1, Pallas kernels: 64.8 us -> 37.6 us  [shards(): pl.pallas_call(functools.partial(layer_kernel, sizes, cells, lengths, scr...]
    unnamed x22 -> x4, local copies, waits for them, and re-layouts: 4.37 us -> 2.16 us
    dot_general x3 -> x0, matrix products: 2.12 us -> none  [the longest x1 1.06 us: shards(): charge = base_charge + jnp.dot(hidden, w_charge, preferred_element_type=f32)]
    reshape x6 -> x0, local copies, waits for them, and re-layouts: 1.81 us -> none  [the longest x1 0.7 us: shards(): site_potential.reshape(cells_x, cells_y, cells_z, slot_count)]
    add x3 -> x0, other arithmetic: 1.2 us -> none  [the longest x1 0.78 us: shards(): code = code.reshape(cell_count, slot_count, NBR) + jnp.where(dead, 256, 0)]
    concatenate x2 -> x0, local copies, waits for them, and re-layouts: 0.95 us -> none  [shards(): rows = jnp.concatenate([sent, place_rows], axis=1)]
    eq x1 -> x0, local copies, waits for them, and re-layouts: 0.84 us -> none  [shards(): species_rows[:, None] == kind_ids[None, :]]
where the time goes in v2:
time: 40.6 us; the launch traced here: 40.5 us
  Pallas kernels  37.6 us (93%)
  local copies, waits for them, and re-layouts  2.16 us (5%)
  between operations  0.65 us (2%)
    pallas_call x1, Pallas kernels, shards(): pl.pallas_call(functools.partial(layer_kernel, sizes, cells, lengths, scr...  37.6 us
    unnamed x4, local copies, waits for them, and re-layouts  2.16 us

profile of v2, /device:TPU:1, one launch (start us, length us, event | category | flops | bytes accessed | tf_op | source)
XLA Modules:
  0.0 40.5 jit_solution(2888135783445610286)
XLA Ops:
  0.6 37.6 %fused_layer.1 = (bf16[384,128]{1,0:T(8,128)(2,1)}, f32[48,8]{1,0:T(8,128)}) custom-call(bf16[3,2,8,8,128]{4,3,2,1,0:T(8,128)(2,1)} %feat_ref.1, bf16[384,128]{1,0:T(8,128)(2,1)} %bitcast.7, f32[48,24]{1,0:T(8,128)} %bitcast.11, s32[48,8]{1,0:T(8,128)} %bitcast.12, s32[48,512]{1,0:T(8,128)} %bitcast.8, s32[48,8]{1,0:T(8,128)} %bitcast.13, ...), custom_call_target="tpu_custom_call" | custom-call | tf_op jit(solution)/shard_map/fused_layer/pallas_call | solution.py:732
  38.3 0.0 copy-start
  38.3 1.5 %copy.30 = bf16[3,2,8,8,128]{4,3,2,1,0:T(8,128)(2,1)} copy(bf16[3,2,8,8,128]{4,3,2,1,0:T(8,128)(2,1)} %bitcast.9) | data formatting | bytes 196608
  39.8 0.0 copy-done
  39.9 0.6 %copy.31 = f32[3,2,8,8]{3,2,1,0:T(8,128)} copy(f32[3,2,8,8]{3,2,1,0:T(8,128)S(1)} %bitcast.10) | data formatting | bytes 3072
Async XLA Ops:
  38.3 1.6 %copy-start = (f32[48,8]{1,0:T(8,128)S(1)}, f32[48,8]{1,0:T(8,128)}, u32[]{:S(2)}) copy-start(f32[48,8]{1,0:T(8,128)} %get-tuple-element.5) | copy-start | bytes 4612

commit v3 on v2

--- a/solution.py
+++ b/solution.py
@@ -12,22 +12,14 @@
 NBR = 64
 CELL = 8
 LANES = 128
-STEP_CELLS = 8
-FIRST_PART = 7
+STEP_CELLS = 12
+FIRST_LOADS = (2, 3, 1, 14, 15, 0)
 VMEM_BYTES = 60 * 1024 * 1024
 AXES = ("gx", "gy", "gz")
 
 coulomb_scale = 0.25
 smearing = 1.0
 f32, bf16, i32 = jnp.float32, jnp.bfloat16, jnp.int32
-
-
-def coords_of(index, sizes):
-    return (
-        index // (sizes[1] * sizes[2]),
-        (index // sizes[2]) % sizes[1],
-        index % sizes[2],
-    )
 
 
 def index_of(coords, sizes):
@@ -87,7 +79,7 @@
     table = np.ascontiguousarray(table).astype(np.float32)
     hi = table.astype(jnp.bfloat16)
     lo = (table - hi.astype(np.float32)).astype(jnp.bfloat16)
-    return jnp.asarray(hi), jnp.asarray(lo)
+    return hi, lo
 
 
 def layer_kernel(
@@ -98,33 +90,7 @@
     planes,
     win_x,
     win_y,
-    feat_ref,
-    hidden_ref,
-    pos_ref,
-    kind_ref,
-    nbr_ref,
-    count_ref,
-    ws_ref,
-    wn_ref,
-    wr_ref,
-    rates_ref,
-    w1_ref,
-    w2_ref,
-    wv_ref,
-    wo_ref,
-    wc_ref,
-    kinds_ref,
-    zrow_ref,
-    krow_ref,
-    kx_ref,
-    by_h_ref,
-    by_l_ref,
-    byt_h_ref,
-    byt_l_ref,
-    bxt_h_ref,
-    bxt_l_ref,
-    bxq_h_ref,
-    bxq_l_ref,
+    sources,
     out_ref,
     site_ref,
     atoms_ref,
@@ -146,6 +112,8 @@
     along_ref,
     field_ref,
     wave_ref,
+    taps_ref,
+    scaled_ref,
     xs_ref,
     ys_ref,
     part_ref,
@@ -160,7 +128,43 @@
     hrecv,
     psend,
     precv,
+    entered,
+    stage_sem,
+    *staged,
 ):
+    (
+        feat_ref,
+        hidden_ref,
+        pos_ref,
+        kind_ref,
+        nbr_ref,
+        count_ref,
+        ws_ref,
+        wn_ref,
+        wr_ref,
+        rates_ref,
+        w1_ref,
+        w2_ref,
+        wv_ref,
+        wo_ref,
+        wc_ref,
+        kinds_ref,
+        zrow_ref,
+        krow_ref,
+        kx_ref,
+        by_ref,
+        byt_ref,
+        bxt_h_ref,
+        bxt_l_ref,
+        bxq_h_ref,
+        bxq_l_ref,
+    ) = staged
+    loads = [
+        pltpu.make_async_copy(source, target, stage_sem.at[k])
+        for k, (source, target) in enumerate(zip(sources, staged))
+    ]
+    for k in FIRST_LOADS:
+        loads[k].start()
     size_x, size_y, size_z = sizes
     cells_x, cells_y, cells_z = cells
     length_x, length_y, length_z = lengths
@@ -195,11 +199,19 @@
             for at, step, size in zip(here, offset, sizes)
         )
 
+    def greet(semaphore):
+        for offset in offsets[:close_count]:
+            pl.semaphore_signal(
+                semaphore, inc=1, device_id=moved(offset, 1), device_id_type=pl.DeviceIdType.MESH
+            )
+
     barrier = pltpu.get_barrier_semaphore()
-    for offset in offsets:
-        pl.semaphore_signal(
-            barrier, inc=1, device_id=moved(offset, 1), device_id_type=pl.DeviceIdType.MESH
-        )
+    greet(barrier)
+    for k in range(len(loads)):
+        if k not in FIRST_LOADS:
+            loads[k].start()
+    for k in FIRST_LOADS:
+        loads[k].wait()
 
     pad_rows = jnp.zeros((LANES - cell_count, 1), f32)
     kinds = kind_ref[...].astype(f32)
@@ -229,8 +241,7 @@
             charge = charge + jnp.where(kind == float(k), kinds_ref[k], 0.0)
         atoms_ref[3:4, where_to] = charge
 
-    def atom_copy(offset, peer, slot):
-        at = index_of(offset, sizes)
+    def atom_copy(at, peer, slot):
         return pltpu.make_async_remote_copy(
             src_ref=atoms_ref,
             dst_ref=all_ref.at[slot],
@@ -239,11 +250,6 @@
             device_id=peer,
             device_id_type=pl.DeviceIdType.MESH,
         )
-
-    def wait_atoms(some):
-        for offset in some:
-            origin = moved(offset, -1)
-            atom_copy(offset, origin, index_of(origin, sizes)).wait()
 
     copies = []
     for shift in range(27):
@@ -275,14 +281,19 @@
                 device_id_type=pl.DeviceIdType.MESH,
             )
         )
-    pl.semaphore_wait(barrier, devices - 1)
+    pl.semaphore_wait(barrier, close_count)
     for offset in offsets[:close_count]:
-        atom_copy(offset, moved(offset, 1), me).start()
+        atom_copy(index_of(offset, sizes), moved(offset, 1), me).start()
+    rounds = max(size // 2 for size in sizes) - 1
+    if rounds > 0:
+        greet(entered.at[0])
     for copy in copies:
         copy.start()
-    for offset in offsets[close_count:]:
-        atom_copy(offset, moved(offset, 1), me).start()
     all_ref[me] = atoms_ref[...]
+
+    for k in range(len(loads)):
+        if k not in FIRST_LOADS:
+            loads[k].wait()
 
     own = mm(hidden_ref[...], ws_ref[...]) * 0.5
     own_hi = own.astype(bf16).astype(f32)
@@ -310,14 +321,17 @@
         gap = jnp.where(gap > 1, gap - total, gap)
         steps.append(jnp.where(gap < -1, gap + total, gap))
     which = ((steps[0] + 1) * 3 + steps[1] + 1) * (3 * slots) + (steps[2] + 1) * slots + slot_id
-    which_ref[...] = which.astype(f32)
-    zlane_ref[...] = ((row_z + steps[2]) * slots + slot_id) & (LANES - 1)
-    column_ref[...] = (steps[0] + 1) * wide_y + row_y + 1 + steps[1]
+    octets = which_ref.shape
+    which_ref[...] = which.astype(f32).reshape(octets)
+    zlane = ((row_z + steps[2]) * slots + slot_id) & (LANES - 1)
+    zlane_ref[...] = zlane.reshape(octets)
+    column = (steps[0] + 1) * wide_y + row_y + 1 + steps[1]
+    column_ref[...] = column.reshape(octets)
     lane_pair = iota((slots, pairs), 1)
     sel = jnp.where(lane_pair // NBR == iota((slots, pairs), 0), 1.0, 0.0)
     limit = mm(count_ref[...].astype(f32).astype(bf16), sel.astype(bf16))
     order = (iota((1, pairs), 1) % NBR).astype(f32)
-    live_ref[...] = jnp.where(order < limit, 1.0, 0.0)
+    live_ref[...] = jnp.where(order < limit, 1.0, 0.0).reshape(octets)
 
     zrow = zrow_ref[me]
     kcol = krow_ref[...]
@@ -335,7 +349,15 @@
         angle = (turns - 0.5 * length_z) * (2.0 * math.pi / length_z)
         ztab_ref[z] = -jnp.cos(angle) * zrow[:, 1:2] - jnp.sin(angle) * zrow[:, 2:3]
 
-    wait_atoms(offsets[:close_count])
+    for r in range(rounds):
+        pl.semaphore_wait(entered.at[r], close_count)
+        if r + 1 < rounds:
+            greet(entered.at[r + 1])
+    for offset in offsets[close_count:]:
+        atom_copy(index_of(offset, sizes), moved(offset, 1), me).start()
+    for offset in offsets[:close_count]:
+        origin = moved(offset, -1)
+        atom_copy(index_of(offset, sizes), origin, index_of(origin, sizes)).wait()
 
     lane4 = iota((4, LANES), 1)
     for x in range(cells_x + 2):
@@ -389,21 +411,20 @@
     sub_y = sub8 // 4
 
     def geometry(octet, carry):
-        rows = pl.ds(pl.multiple_of(octet * 8, 8), 8)
         for r in range(8):
-            place_cell(octet * 8 + r, rows, r)
+            place_cell(octet * 8 + r, octet, r)
         return carry
 
-    def place_cell(c, rows, r):
+    def place_cell(c, octet, r):
         cz = lax.rem(c, cells_z)
         cxy = c // cells_z
         cx = cxy // cells_y
         for chunk in range(pairs // LANES):
             part = pl.ds(chunk * LANES, LANES)
-            spot = jnp.broadcast_to(zlane_ref[rows, part][r : r + 1], (slots, LANES))
-            column = jnp.broadcast_to(column_ref[rows, part][r : r + 1], (slots, LANES)) - sub_y
-            live = live_ref[rows, part][r : r + 1]
-            which = which_ref[rows, part][r : r + 1]
+            spot = jnp.broadcast_to(zlane_ref[octet, r : r + 1, part], (slots, LANES))
+            column = jnp.broadcast_to(column_ref[octet, r : r + 1, part], (slots, LANES)) - sub_y
+            live = live_ref[octet, r : r + 1, part]
+            which = which_ref[octet, r : r + 1, part]
             found = jnp.zeros((slots, LANES), f32)
             for dx in range(3):
                 for pair_y in range(wide_y // 2):
@@ -502,16 +523,25 @@
                 vec_ref[d, mine, :] = rest[1 + 2 * d] + rest[2 + 2 * d]
         return carry
 
-    first_steps = cell_count // STEP_CELLS * FIRST_PART // 16
-    lax.fori_loop(0, first_steps, pair_step, 0)
-    wait_atoms(offsets[close_count:])
-
     lanes = size_z * atom_count
 
-    def spread(g, carry):
-        gx = g // size_y
-        gy = lax.rem(g, size_y)
+    def spread(turn, carry):
+        gx = lax.rem(here[0] + size_x - turn // size_y, size_x)
+        gy = lax.rem(here[1] + size_y - lax.rem(turn, size_y), size_y)
+        g = gx * size_y + gy
         base = g * size_z
+        step_x, step_y = turn // size_y, lax.rem(turn, size_y)
+        far_group = jnp.logical_or(
+            jnp.logical_and(step_x > 1, step_x < size_x - 1),
+            jnp.logical_and(step_y > 1, step_y < size_y - 1),
+        )
+        for z in range(size_z):
+            gz = lax.rem(here[2] + size_z - z, size_z)
+            copy = atom_copy(turn * size_z + z, (gx, gy, gz), base + gz)
+            if z in (0, 1, size_z - 1):
+                pl.when(far_group)(copy.wait)
+            else:
+                copy.wait()
         atoms = jnp.concatenate([all_ref[base + i] for i in range(size_z)], axis=1)
         whole = jnp.floor(atoms)
         f = atoms - whole
@@ -524,30 +554,33 @@
             (-3.0 * cube + 3.0 * sq + 3.0 * f + 1.0) * (1.0 / 6.0),
             cube * (1.0 / 6.0),
         ]
+        for t in range(4):
+            taps_ref[t] = taps[t]
+        taps_ref[4] = whole
         first_x = (gx * (cells_x * CELL)).astype(f32)
         first_y = (gy * (cells_y * CELL)).astype(f32)
-        off_x = iota((win_x, 1), 0).astype(f32).astype(bf16) - (whole[0:1] - first_x).astype(bf16)
+        off_x = iota((win_x, 1), 0).astype(f32).astype(bf16) - (taps_ref[4, 0:1, :] - first_x).astype(bf16)
         x_hi = jnp.zeros((win_x, lanes), bf16)
         x_lo = jnp.zeros((win_x, lanes), bf16)
         for t in range(4):
             hit = off_x == jnp.asarray(t, bf16)
-            t_hi, t_lo = two_pieces(taps[t][0:1])
+            t_hi, t_lo = two_pieces(taps_ref[t, 0:1, :])
             x_hi = jnp.where(hit, jnp.broadcast_to(t_hi, hit.shape), x_hi)
             x_lo = jnp.where(hit, jnp.broadcast_to(t_lo, hit.shape), x_lo)
-        off_y = iota((win_y, 1), 0).astype(f32) - (whole[1:2] - first_y)
+        off_y = iota((win_y, 1), 0).astype(f32) - (taps_ref[4, 1:2, :] - first_y)
         rows_y = jnp.zeros((win_y, lanes), f32)
         for t in range(4):
-            rows_y = jnp.where(off_y == float(t), taps[t][1:2], rows_y)
+            rows_y = jnp.where(off_y == float(t), taps_ref[t, 1:2, :], rows_y)
         waves = []
         for z in range(size_z):
             table = ztab_ref[z]
             for chunk in range(atom_count // LANES):
                 part = slice(z * atom_count + chunk * LANES, z * atom_count + (chunk + 1) * LANES)
-                spot = (whole[2:3, part] - float(z * cells_z * CELL)).astype(i32)
+                spot = (taps_ref[4, 2:3, part] - float(z * cells_z * CELL)).astype(i32)
                 spot = jnp.broadcast_to(spot, table.shape)
                 wave = None
                 for t in range(4):
-                    term = lane_pick(table, spot + t) * taps[t][2:3, part]
+                    term = lane_pick(table, spot + t) * taps_ref[t, 2:3, part]
                     wave = term if wave is None else wave + term
                 waves.append(wave)
         wave = jnp.concatenate(waves, axis=1)
@@ -555,8 +588,8 @@
         ys_ref[g] = rows_y
         rows_x = jnp.concatenate([x_hi, x_lo], axis=0)
         xs_ref[g] = rows_x
-        scaled = wave * atoms[3:4]
-        left = jnp.concatenate([rows_y * scaled[j : j + 1] for j in range(planes)], axis=0)
+        scaled_ref[...] = wave * atoms[3:4]
+        left = jnp.concatenate([rows_y * scaled_ref[j : j + 1, :] for j in range(planes)], axis=0)
         l_hi, l_lo = two_pieces(left)
         res = mm_nt(l_hi, rows_x) + mm_nt(l_lo, rows_x)
         per_block = LANES // (2 * win_x)
@@ -571,37 +604,43 @@
 
     spectrum = None
     for block in range(plane_ref.shape[0]):
-        for j in range(planes):
-            p_hi, p_lo = two_pieces(plane_ref[block, j])
-            along_ref[j * length_y : (j + 1) * length_y, :] = (
-                mm(by_h_ref[...], p_hi) + mm(by_h_ref[...], p_lo) + mm(by_l_ref[...], p_hi)
+        for j in range(0, planes, 2):
+            p_hi, p_lo = two_pieces(
+                jnp.concatenate([plane_ref[block, j], plane_ref[block, j + 1]], axis=1)
             )
+            both = mm(by_ref[0], p_hi) + mm(by_ref[0], p_lo) + mm(by_ref[1], p_hi)
+            along_ref[j * length_y : (j + 1) * length_y, :] = both[:, :LANES]
+            along_ref[(j + 1) * length_y : (j + 2) * length_y, :] = both[:, LANES:]
         a_hi, a_lo = two_pieces(along_ref[...])
-        part = mm(a_hi, bxt_h_ref[block]) + mm(a_lo, bxt_h_ref[block]) + mm(a_hi, bxt_l_ref[block])
+        bxt_h = bxt_h_ref[block]
+        part = mm(jnp.concatenate([a_hi, a_lo], axis=1), jnp.concatenate([bxt_h, bxt_h], axis=0))
+        part = part + mm(a_hi, bxt_l_ref[block])
         spectrum = part if spectrum is None else spectrum + part
     s_hi, s_lo = two_pieces(spectrum * green_ref[...])
-    lane_x = iota((1, LANES), 1) % (2 * win_x) < win_x
-    for gx in range(size_x):
-        cols = slice(gx * LANES, (gx + 1) * LANES)
-        back = mm(s_hi, bxq_h_ref[:, cols]) + mm(s_lo, bxq_h_ref[:, cols]) + mm(s_hi, bxq_l_ref[:, cols])
+    lane_x = iota((1, 2 * LANES), 1) % (2 * win_x) < win_x
+    for gx in range(0, size_x, 2):
+        cols = slice(gx * LANES, (gx + 2) * LANES)
+        back = (
+            mm(s_hi, bxq_h_ref[:, cols]) + mm(s_lo, bxq_h_ref[:, cols]) + mm(s_hi, bxq_l_ref[:, cols])
+        )
         b_hi, b_lo = two_pieces(back)
         for j in range(planes):
             rows = slice(j * length_y, (j + 1) * length_y)
-            value = (
-                mm(byt_h_ref[...], b_hi[rows])
-                + mm(byt_h_ref[...], b_lo[rows])
-                + mm(byt_l_ref[...], b_hi[rows])
+            value = mm(
+                byt_ref[...], jnp.concatenate([b_hi[rows], b_lo[rows], b_hi[rows]], axis=0)
             )
             v_hi = value.astype(bf16).astype(f32)
-            field_ref[gx, j] = jnp.where(lane_x, v_hi, value - v_hi)
+            value = jnp.where(lane_x, v_hi, value - v_hi)
+            field_ref[gx, j] = value[:, :LANES]
+            field_ref[gx + 1, j] = value[:, LANES:]
 
     def part_copy(o, peer):
         return pltpu.make_async_remote_copy(
-            src_ref=part_ref.at[peer],
+            src_ref=part_ref.at[index_of(peer, sizes)],
             dst_ref=held_ref.at[o],
             send_sem=psend.at[o],
             recv_sem=precv.at[o],
-            device_id=coords_of(peer, sizes),
+            device_id=peer,
             device_id_type=pl.DeviceIdType.MESH,
         )
 
@@ -614,44 +653,45 @@
         x_lo = xs_ref[g, win_x:]
         stack = [x_hi, x_hi, x_lo, x_lo] + [jnp.zeros_like(x_hi)] * (LANES // win_x - 4)
         values = mm(field.astype(bf16), jnp.concatenate(stack, axis=0))
-        wave = wave_ref[g]
-        mixed = values[0:win_y] * wave[0:1]
+        mixed = values[0:win_y] * wave_ref[g, 0:1, :]
         for j in range(1, planes):
-            mixed = mixed + values[j * win_y : (j + 1) * win_y] * wave[j : j + 1]
+            mixed = mixed + values[j * win_y : (j + 1) * win_y] * wave_ref[g, j : j + 1, :]
         line = jnp.sum(mixed * ys_ref[g], axis=0, keepdims=True)
         for i in range(size_z):
             part_ref[g * size_z + i] = line[:, i * atom_count : (i + 1) * atom_count]
         return carry
 
-    lax.fori_loop(0, size_x * size_y, sample, 0)
-
-    def send(o, carry):
-        part_copy(o, lax.rem(me + o, devices)).start()
-        return carry
-
-    lax.fori_loop(1, devices, send, 0)
-
-    lax.fori_loop(first_steps, cell_count // STEP_CELLS, pair_step, 0)
-
+    lax.fori_loop(0, size_x * size_y, sample, 0, unroll=4)
+
+    for offset in offsets:
+        part_copy(index_of(offset, sizes), moved(offset, 1)).start()
+
+    lax.fori_loop(0, cell_count // STEP_CELLS, pair_step, 0)
+
+    wv_twice = jnp.concatenate([wv_ref[...], wv_ref[...]], axis=0)
     invariant = None
     for d in range(3):
-        v_hi, v_lo = two_pieces(vec_ref[d])
-        vector = (mm(v_hi, wv_ref[...]) + mm(v_lo, wv_ref[...])) * (1.0 / math.sqrt(NBR))
+        vector = mm(jnp.concatenate(two_pieces(vec_ref[d]), axis=1), wv_twice)
+        vector = vector * (1.0 / math.sqrt(NBR))
         part = vector * vector
         invariant = part if invariant is None else invariant + part
     update = (msg_ref[...] + invariant).astype(bf16)
     out_ref[...] = (hidden_ref[...].astype(f32) + mm(update, wo_ref[...])).astype(bf16)
 
-    def take(o, total):
-        part_copy(o, lax.rem(me + o, devices)).wait()
-        return total + held_ref[o]
-
-    total = lax.fori_loop(1, devices, take, part_ref[me])
+    for offset in offsets:
+        part_copy(index_of(offset, sizes), moved(offset, 1)).wait()
+    held_ref[0] = part_ref[me]
+    total = jnp.sum(held_ref[...], axis=0)
     rows = LANES // slots
     spot = iota((rows, LANES), 0) * slots + lax.rem(iota((rows, LANES), 1), slots)
     for chunk in range(atom_count // LANES):
         line = jnp.broadcast_to(total[:, chunk * LANES : (chunk + 1) * LANES], (rows, LANES))
         site_ref[chunk * rows : (chunk + 1) * rows, :] = lane_pick(line, spot)[:, :slots]
+
+
+def staged_kernel(*args):
+    count = args[7]
+    layer_kernel(*args[:7], args[8 : 8 + count], *args[8 + count :])
 
 
 def shards(
@@ -720,63 +760,14 @@
         forward[g // per_block, at : at + 2 * win_x] = np.concatenate([cols, cols], axis=1).T
         backward[:, g * LANES : g * LANES + 4 * win_x] = np.concatenate([cols] * 4, axis=1)
     tables = [jnp.asarray(zrow), jnp.asarray(krow), jnp.asarray(kx)]
-    for table in (by, by.T, forward, backward):
+    by_hi, by_lo = host_pieces(by)
+    tables.append(np.stack([by_hi, by_lo]))
+    tables.append(np.concatenate([by_hi.T, by_hi.T, by_lo.T], axis=1))
+    for table in (forward, backward):
         tables += host_pieces(table)
-
-    vmem = pl.BlockSpec(memory_space=pltpu.VMEM)
-    smem = pl.BlockSpec(memory_space=pltpu.SMEM)
-    dma = pltpu.SemaphoreType.DMA
-    groups = sizes[0] * sizes[1]
-    lanes = sizes[2] * atom_count
-    columns = (cells_x + 2) * (cells_y + 2)
-    updated, site_potential = pl.pallas_call(
-        functools.partial(layer_kernel, sizes, cells, lengths, screen, planes, win_x, win_y),
-        out_shape=(
-            jax.ShapeDtypeStruct((atom_count, channels), bf16),
-            jax.ShapeDtypeStruct((cell_count, slot_count), f32),
-        ),
-        in_specs=[vmem] * 9 + [smem] + [vmem] * 5 + [smem] + [vmem] * 11,
-        out_specs=(vmem, vmem),
-        scratch_shapes=[
-            pltpu.VMEM((4, atom_count), f32),
-            pltpu.VMEM((devices, 4, atom_count), f32),
-            pltpu.VMEM(tuple(c + 2 for c in cells) + (slot_count, channels), bf16),
-            pltpu.VMEM((columns, (cells_z + 2) * slot_count, channels), f32),
-            pltpu.VMEM((2, atom_count, channels), f32),
-            pltpu.VMEM((cell_count, pairs), f32),
-            pltpu.VMEM((cell_count, pairs), i32),
-            pltpu.VMEM((cell_count, pairs), i32),
-            pltpu.VMEM((cell_count, pairs), f32),
-            pltpu.VMEM((planes * length_y, length_x), f32),
-            pltpu.VMEM((columns // 2, 8, LANES), f32),
-            pltpu.VMEM((cells_x * cells_y, 8, LANES), f32),
-            pltpu.VMEM((cell_count, 8, pairs), f32),
-            pltpu.VMEM((cell_count, 8, pairs), f32),
-            pltpu.VMEM((sizes[2], plane_rows, LANES), f32),
-            pltpu.VMEM((blocks, planes, sizes[1] * win_y, LANES), f32),
-            pltpu.VMEM((planes * length_y, LANES), f32),
-            pltpu.VMEM((sizes[0], planes, sizes[1] * win_y, LANES), f32),
-            pltpu.VMEM((groups, plane_rows, lanes), f32),
-            pltpu.VMEM((groups, 2 * win_x, lanes), bf16),
-            pltpu.VMEM((groups, win_y, lanes), f32),
-            pltpu.VMEM((devices, 1, atom_count), f32),
-            pltpu.VMEM((devices, 1, atom_count), f32),
-            pltpu.VMEM((atom_count, channels), f32),
-            pltpu.VMEM((3, atom_count, channels), f32),
-            pltpu.VMEM((2 * channels, 2 * channels), bf16),
-            pltpu.VMEM((2 * channels, 2 * channels), bf16),
-            dma((devices,)),
-            dma((devices,)),
-            dma((27,)),
-            dma((27,)),
-            dma((devices,)),
-            dma((devices,)),
-        ],
-        name="fused_layer",
-        compiler_params=pltpu.CompilerParams(
-            has_side_effects=True, collective_id=0, vmem_limit_bytes=VMEM_BYTES
-        ),
-    )(
+    tables = [jnp.asarray(t) for t in tables]
+
+    operands = (
         features,
         features.reshape(atom_count, channels),
         positions.reshape(cell_count, 3 * slot_count),
@@ -795,6 +786,71 @@
         species_charge,
         *tables,
     )
+    vmem = pl.BlockSpec(memory_space=pltpu.VMEM)
+    dma = pltpu.SemaphoreType.DMA
+    groups = sizes[0] * sizes[1]
+    lanes = sizes[2] * atom_count
+    columns = (cells_x + 2) * (cells_y + 2)
+    updated, site_potential = pl.pallas_call(
+        functools.partial(
+            staged_kernel, sizes, cells, lengths, screen, planes, win_x, win_y, len(operands)
+        ),
+        out_shape=(
+            jax.ShapeDtypeStruct((atom_count, channels), bf16),
+            jax.ShapeDtypeStruct((cell_count, slot_count), f32),
+        ),
+        in_specs=[pl.BlockSpec(memory_space=pl.ANY)] * len(operands),
+        out_specs=(vmem, vmem),
+        scratch_shapes=[
+            pltpu.VMEM((4, atom_count), f32),
+            pltpu.VMEM((devices, 4, atom_count), f32),
+            pltpu.VMEM(tuple(c + 2 for c in cells) + (slot_count, channels), bf16),
+            pltpu.VMEM((columns, (cells_z + 2) * slot_count, channels), f32),
+            pltpu.VMEM((2, atom_count, channels), f32),
+            pltpu.VMEM((cell_count // 8, 8, pairs), f32),
+            pltpu.VMEM((cell_count // 8, 8, pairs), i32),
+            pltpu.VMEM((cell_count // 8, 8, pairs), i32),
+            pltpu.VMEM((cell_count // 8, 8, pairs), f32),
+            pltpu.VMEM((planes * length_y, length_x), f32),
+            pltpu.VMEM((columns // 2, 8, LANES), f32),
+            pltpu.VMEM((cells_x * cells_y, 8, LANES), f32),
+            pltpu.VMEM((cell_count, 8, pairs), f32),
+            pltpu.VMEM((cell_count, 8, pairs), f32),
+            pltpu.VMEM((sizes[2], plane_rows, LANES), f32),
+            pltpu.VMEM((blocks, planes, sizes[1] * win_y, LANES), f32),
+            pltpu.VMEM((planes * length_y, LANES), f32),
+            pltpu.VMEM((sizes[0], planes, sizes[1] * win_y, LANES), f32),
+            pltpu.VMEM((groups, plane_rows, lanes), f32),
+            pltpu.VMEM((5, 4, lanes), f32),
+            pltpu.VMEM((plane_rows, lanes), f32),
+            pltpu.VMEM((groups, 2 * win_x, lanes), bf16),
+            pltpu.VMEM((groups, win_y, lanes), f32),
+            pltpu.VMEM((devices, 1, atom_count), f32),
+            pltpu.VMEM((devices, 1, atom_count), f32),
+            pltpu.VMEM((atom_count, channels), f32),
+            pltpu.VMEM((3, atom_count, channels), f32),
+            pltpu.VMEM((2 * channels, 2 * channels), bf16),
+            pltpu.VMEM((2 * channels, 2 * channels), bf16),
+            dma((devices,)),
+            dma((devices,)),
+            dma((27,)),
+            dma((27,)),
+            dma((devices,)),
+            dma((devices,)),
+            pltpu.SemaphoreType.REGULAR((max(max(size // 2 for size in sizes) - 1, 1),)),
+            dma((len(operands),)),
+        ]
+        + [
+            (pltpu.SMEM if a is radial_rates or a is species_charge else pltpu.VMEM)(
+                a.shape, a.dtype
+            )
+            for a in operands
+        ],
+        name="fused_layer",
+        compiler_params=pltpu.CompilerParams(
+            has_side_effects=True, collective_id=0, vmem_limit_bytes=VMEM_BYTES
+        ),
+    )(*operands)
     return (
         updated.reshape(features.shape),
         site_potential.reshape(cells_x, cells_y, cells_z, slot_count),

time: 40.6 us -> 37.4 us (0.921)
  Pallas kernels: 37.6 us -> 34.5 us
    pallas_call x1, Pallas kernels: 37.6 us -> 34.5 us  [shards(): pl.pallas_call(functools.partial(staged_kernel, sizes, cells, lengths, sc...]
where the time goes in v3:
time: 37.4 us; the launch traced here: 37.3 us
  Pallas kernels  34.5 us (92%)
  local copies, waits for them, and re-layouts  2.16 us (6%)
  between operations  0.65 us (2%)
    pallas_call x1, Pallas kernels, shards(): pl.pallas_call(functools.partial(staged_kernel, sizes, cells, lengths, sc...  34.5 us
    unnamed x4, local copies, waits for them, and re-layouts  2.16 us

profile of v3, /device:TPU:1, one launch (start us, length us, event | category | flops | bytes accessed | tf_op | source)
XLA Modules:
  0.0 37.3 jit_solution(15278336470025832197)
XLA Ops:
  0.6 34.5 %fused_layer.1 = (bf16[384,128]{1,0:T(8,128)(2,1)}, f32[48,8]{1,0:T(8,128)}) custom-call(bf16[3,2,8,8,128]{4,3,2,1,0:T(8,128)(2,1)} %args_0_.4, bf16[384,128]{1,0:T(8,128)(2,1)} %bitcast.7, f32[48,24]{1,0:T(8,128)} %bitcast.11, s32[48,8]{1,0:T(8,128)} %bitcast.12, s32[48,512]{1,0:T(8,128)} %bitcast.8, s32[48,8]{1,0:T(8,128)} %bitcast.13, ...), custom_call_target="tpu_custom_call" | custom-call | tf_op jit(solution)/shard_map/fused_layer/pallas_call | solution.py:794
  35.1 0.0 copy-start
  35.1 1.5 %copy.28 = bf16[3,2,8,8,128]{4,3,2,1,0:T(8,128)(2,1)} copy(bf16[3,2,8,8,128]{4,3,2,1,0:T(8,128)(2,1)} %bitcast.9) | data formatting | bytes 196608
  36.7 0.0 copy-done
  36.7 0.6 %copy.29 = f32[3,2,8,8]{3,2,1,0:T(8,128)} copy(f32[3,2,8,8]{3,2,1,0:T(8,128)S(1)} %bitcast.10) | data formatting | bytes 3072
Async XLA Ops:
  35.1 1.6 %copy-start = (f32[48,8]{1,0:T(8,128)S(1)}, f32[48,8]{1,0:T(8,128)}, u32[]{:S(2)}) copy-start(f32[48,8]{1,0:T(8,128)} %get-tuple-element.5) | copy-start | bytes 4612

commit v4 on v3

--- a/solution.py
+++ b/solution.py
@@ -52,7 +52,16 @@
 
 
 def lane_pick(table, index):
-    return jnp.take_along_axis(table, index, axis=1)
+    dims = lax.GatherDimensionNumbers(
+        offset_dims=(),
+        collapsed_slice_dims=(1,),
+        start_index_map=(1,),
+        operand_batching_dims=(0,),
+        start_indices_batching_dims=(0,),
+    )
+    return lax.gather(
+        table, index[..., None], dims, (1, 1), mode=lax.GatherScatterMode.PROMISE_IN_BOUNDS
+    )
 
 
 def silu_of_half(half):
@@ -441,7 +450,7 @@
             reach = jnp.where(row_d == 3, 1.0, scaled) * live
             reach_ref[c, :, part] = jnp.where(row_d == 4, which, reach)
 
-    lax.fori_loop(0, cell_count // 8, geometry, 0)
+    lax.fori_loop(0, cell_count // 8, geometry, 0, unroll=2)
 
     for copy in copies:
         copy.wait()
@@ -524,6 +533,7 @@
         return carry
 
     lanes = size_z * atom_count
+    body_y = win_y - 8
 
     def spread(turn, carry):
         gx = lax.rem(here[0] + size_x - turn // size_y, size_x)
@@ -559,15 +569,27 @@
         taps_ref[4] = whole
         first_x = (gx * (cells_x * CELL)).astype(f32)
         first_y = (gy * (cells_y * CELL)).astype(f32)
-        off_x = iota((win_x, 1), 0).astype(f32).astype(bf16) - (taps_ref[4, 0:1, :] - first_x).astype(bf16)
-        x_hi = jnp.zeros((win_x, lanes), bf16)
-        x_lo = jnp.zeros((win_x, lanes), bf16)
+        tiles = win_x // 16
+
+        def packed(row):
+            wide = jnp.broadcast_to(row, (16, lanes))
+            hi = wide.astype(bf16)
+            return [hi, (wide - hi.astype(f32)).astype(bf16)]
+
+        start_x = packed(taps_ref[4, 0:1, :] - first_x)[0]
+        off_x = [(iota((16, 1), 0) + 16 * i).astype(f32).astype(bf16) - start_x for i in range(tiles)]
+        none = jnp.zeros((16, lanes), bf16)
+        x_hi = [none] * tiles
+        x_lo = [none] * tiles
         for t in range(4):
-            hit = off_x == jnp.asarray(t, bf16)
-            t_hi, t_lo = two_pieces(taps_ref[t, 0:1, :])
-            x_hi = jnp.where(hit, jnp.broadcast_to(t_hi, hit.shape), x_hi)
-            x_lo = jnp.where(hit, jnp.broadcast_to(t_lo, hit.shape), x_lo)
-        off_y = iota((win_y, 1), 0).astype(f32) - (taps_ref[4, 1:2, :] - first_y)
+            t_hi, t_lo = packed(taps_ref[t, 0:1, :])
+            for i in range(tiles):
+                hit = off_x[i] == jnp.asarray(t, bf16)
+                x_hi[i] = jnp.where(hit, t_hi, x_hi[i])
+                x_lo[i] = jnp.where(hit, t_lo, x_lo[i])
+        row_y = iota((win_y, 1), 0)
+        row_y = jnp.where(row_y < body_y + 4, row_y, row_y - 4).astype(f32)
+        off_y = row_y - (taps_ref[4, 1:2, :] - first_y)
         rows_y = jnp.zeros((win_y, lanes), f32)
         for t in range(4):
             rows_y = jnp.where(off_y == float(t), taps_ref[t, 1:2, :], rows_y)
@@ -586,10 +608,15 @@
         wave = jnp.concatenate(waves, axis=1)
         wave_ref[g] = wave
         ys_ref[g] = rows_y
-        rows_x = jnp.concatenate([x_hi, x_lo], axis=0)
+        rows_x = jnp.concatenate(x_hi + x_lo, axis=0)
         xs_ref[g] = rows_x
         scaled_ref[...] = wave * atoms[3:4]
-        left = jnp.concatenate([rows_y * scaled_ref[j : j + 1, :] for j in range(planes)], axis=0)
+        sub_low = iota((8, 1), 0) < 4
+        left = [rows_y[:body_y] * scaled_ref[j : j + 1, :] for j in range(planes)]
+        for j in range(0, planes, 2):
+            both = jnp.where(sub_low, scaled_ref[j : j + 1, :], scaled_ref[j + 1 : j + 2, :])
+            left.append(rows_y[body_y:] * both)
+        left = jnp.concatenate(left, axis=0)
         l_hi, l_lo = two_pieces(left)
         res = mm_nt(l_hi, rows_x) + mm_nt(l_lo, rows_x)
         per_block = LANES // (2 * win_x)
@@ -597,7 +624,10 @@
         res = pltpu.roll(res, lax.rem(gx, per_block) * (2 * win_x), 1)
         rows = pl.ds(pl.multiple_of(gy * win_y, 8), win_y)
         for j in range(planes):
-            plane_ref[gx // per_block, j, rows, :] += res[j * win_y : (j + 1) * win_y]
+            ends = res[planes * body_y + j // 2 * 8 : planes * body_y + j // 2 * 8 + 8]
+            ends = jnp.where(sub_low if j % 2 == 0 else ~sub_low, ends, 0.0)
+            body = res[j * body_y : (j + 1) * body_y]
+            plane_ref[gx // per_block, j, rows, :] += jnp.concatenate([body, ends], axis=0)
         return carry
 
     lax.fori_loop(0, size_x * size_y, spread, 0)
@@ -648,14 +678,29 @@
         gx = g // size_y
         gy = lax.rem(g, size_y)
         rows = pl.ds(pl.multiple_of(gy * win_y, 8), win_y)
-        field = jnp.concatenate([field_ref[gx, j, rows, :] for j in range(planes)], axis=0)
+        planes_here = [field_ref[gx, j, rows, :] for j in range(planes)]
+        sub_low = iota((8, 1), 0) < 4
+        field = [block[:body_y] for block in planes_here]
+        for j in range(0, planes, 2):
+            field.append(
+                jnp.where(sub_low, planes_here[j][body_y:], planes_here[j + 1][body_y:])
+            )
+        field = jnp.concatenate(field, axis=0)
         x_hi = xs_ref[g, 0:win_x]
         x_lo = xs_ref[g, win_x:]
         stack = [x_hi, x_hi, x_lo, x_lo] + [jnp.zeros_like(x_hi)] * (LANES // win_x - 4)
         values = mm(field.astype(bf16), jnp.concatenate(stack, axis=0))
-        mixed = values[0:win_y] * wave_ref[g, 0:1, :]
-        for j in range(1, planes):
-            mixed = mixed + values[j * win_y : (j + 1) * win_y] * wave_ref[g, j : j + 1, :]
+        body = None
+        ends = None
+        for j in range(planes):
+            term = values[j * body_y : (j + 1) * body_y] * wave_ref[g, j : j + 1, :]
+            body = term if body is None else body + term
+        for j in range(0, planes, 2):
+            at = planes * body_y + j // 2 * 8
+            both = jnp.where(sub_low, wave_ref[g, j : j + 1, :], wave_ref[g, j + 1 : j + 2, :])
+            term = values[at : at + 8] * both
+            ends = term if ends is None else ends + term
+        mixed = jnp.concatenate([body, ends], axis=0)
         line = jnp.sum(mixed * ys_ref[g], axis=0, keepdims=True)
         for i in range(size_z):
             part_ref[g * size_z + i] = line[:, i * atom_count : (i + 1) * atom_count]
@@ -725,8 +770,8 @@
 
     share = length_z // 2 // devices
     planes = 2 * share
-    win_x = -(-(cells_x * CELL + 4) // 8) * 8
-    win_y = -(-(cells_y * CELL + 4) // 8) * 8
+    win_x = -(-(cells_x * CELL + 4) // 16) * 16
+    win_y = cells_y * CELL + 8
     assert 2 * cells_z * slot_count == LANES and cells_y % 2 == 0
     assert LANES % (4 * win_x) == 0 and cells_z * CELL + 4 <= LANES
     all_modes = np.arange(length_z // 2)
@@ -748,7 +793,9 @@
     zrow = zrow.astype(np.float32)
     kx = np.stack([qx, sx]).astype(np.float32)
     grid_x, grid_y = cells_x * CELL, cells_y * CELL
-    at_y = np.concatenate([(np.arange(win_y) + g * grid_y - 1) % length_y for g in range(sizes[1])])
+    row_y = np.arange(win_y)
+    row_y = np.where(row_y < grid_y + 4, row_y, row_y - 4)
+    at_y = np.concatenate([(row_y + g * grid_y - 1) % length_y for g in range(sizes[1])])
     by = basis_y[:, at_y]
     per_block = LANES // (2 * win_x)
     blocks = -(-sizes[0] // per_block)

time: 37.4 us -> 36.4 us (0.973)
  Pallas kernels: 34.5 us -> 33.5 us
    pallas_call x1, Pallas kernels: 34.5 us -> 33.5 us  [shards(): pl.pallas_call(functools.partial(staged_kernel, sizes, cells, lengths, sc...]
where the time goes in v4:
time: 36.4 us; the launch traced here: 36.3 us
  Pallas kernels  33.5 us (92%)
  local copies, waits for them, and re-layouts  2.16 us (6%)
  between operations  0.65 us (2%)
    pallas_call x1, Pallas kernels, shards(): pl.pallas_call(functools.partial(staged_kernel, sizes, cells, lengths, sc...  33.5 us
    unnamed x4, local copies, waits for them, and re-layouts  2.16 us

profile of v4, /device:TPU:1, one launch (start us, length us, event | category | flops | bytes accessed | tf_op | source)
XLA Modules:
  0.0 36.3 jit_solution(1131256875949318278)
XLA Ops:
  0.6 33.5 %fused_layer.1 = (bf16[384,128]{1,0:T(8,128)(2,1)}, f32[48,8]{1,0:T(8,128)}) custom-call(bf16[3,2,8,8,128]{4,3,2,1,0:T(8,128)(2,1)} %args_0_.4, bf16[384,128]{1,0:T(8,128)(2,1)} %bitcast.7, f32[48,24]{1,0:T(8,128)} %bitcast.11, s32[48,8]{1,0:T(8,128)} %bitcast.12, s32[48,512]{1,0:T(8,128)} %bitcast.8, s32[48,8]{1,0:T(8,128)} %bitcast.13, ...), custom_call_target="tpu_custom_call" | custom-call | tf_op jit(solution)/shard_map/fused_layer/pallas_call | solution.py:841
  34.1 0.0 copy-start
  34.1 1.5 %copy.28 = bf16[3,2,8,8,128]{4,3,2,1,0:T(8,128)(2,1)} copy(bf16[3,2,8,8,128]{4,3,2,1,0:T(8,128)(2,1)} %bitcast.9) | data formatting | bytes 196608
  35.7 0.0 copy-done
  35.7 0.6 %copy.29 = f32[3,2,8,8]{3,2,1,0:T(8,128)} copy(f32[3,2,8,8]{3,2,1,0:T(8,128)S(1)} %bitcast.10) | data formatting | bytes 3072
Async XLA Ops:
  34.1 1.6 %copy-start = (f32[48,8]{1,0:T(8,128)S(1)}, f32[48,8]{1,0:T(8,128)}, u32[]{:S(2)}) copy-start(f32[48,8]{1,0:T(8,128)} %get-tuple-element.5) | copy-start | bytes 4612

commit v5 on v4

--- a/solution.py
+++ b/solution.py
@@ -706,7 +706,7 @@
             part_ref[g * size_z + i] = line[:, i * atom_count : (i + 1) * atom_count]
         return carry
 
-    lax.fori_loop(0, size_x * size_y, sample, 0, unroll=4)
+    lax.fori_loop(0, size_x * size_y, sample, 0, unroll=8)
 
     for offset in offsets:
         part_copy(index_of(offset, sizes), moved(offset, 1)).start()

time: 36.4 us -> 36.1 us (level)
  no operation moved by 1% of the time
where the time goes in v5:
time: 36.1 us; the launch traced here: 36 us
  Pallas kernels  33.2 us (92%)
  local copies, waits for them, and re-layouts  2.16 us (6%)
  between operations  0.65 us (2%)
    pallas_call x1, Pallas kernels, shards(): pl.pallas_call(functools.partial(staged_kernel, sizes, cells, lengths, sc...  33.2 us
    unnamed x4, local copies, waits for them, and re-layouts  2.16 us

profile of v5, /device:TPU:1, one launch (start us, length us, event | category | flops | bytes accessed | tf_op | source)
XLA Modules:
  0.0 36.0 jit_solution(204164873429229123)
XLA Ops:
  0.6 33.2 %fused_layer.1 = (bf16[384,128]{1,0:T(8,128)(2,1)}, f32[48,8]{1,0:T(8,128)}) custom-call(bf16[3,2,8,8,128]{4,3,2,1,0:T(8,128)(2,1)} %args_0_.4, bf16[384,128]{1,0:T(8,128)(2,1)} %bitcast.7, f32[48,24]{1,0:T(8,128)} %bitcast.11, s32[48,8]{1,0:T(8,128)} %bitcast.12, s32[48,512]{1,0:T(8,128)} %bitcast.8, s32[48,8]{1,0:T(8,128)} %bitcast.13, ...), custom_call_target="tpu_custom_call" | custom-call | tf_op jit(solution)/shard_map/fused_layer/pallas_call | solution.py:841
  33.8 0.0 copy-start
  33.8 1.5 %copy.28 = bf16[3,2,8,8,128]{4,3,2,1,0:T(8,128)(2,1)} copy(bf16[3,2,8,8,128]{4,3,2,1,0:T(8,128)(2,1)} %bitcast.9) | data formatting | bytes 196608
  35.4 0.0 copy-done
  35.4 0.6 %copy.29 = f32[3,2,8,8]{3,2,1,0:T(8,128)} copy(f32[3,2,8,8]{3,2,1,0:T(8,128)S(1)} %bitcast.10) | data formatting | bytes 3072
Async XLA Ops:
  33.8 1.6 %copy-start = (f32[48,8]{1,0:T(8,128)S(1)}, f32[48,8]{1,0:T(8,128)}, u32[]{:S(2)}) copy-start(f32[48,8]{1,0:T(8,128)} %get-tuple-element.5) | copy-start | bytes 4612
